TPU v7x, 256 devices: a whole 4x4x8 slice. The times are simulated.
256 devices in a mesh: depth: 8 (over z), col: 4 (over y), row: 8 (over x, core).
Axes of the slice: x: 4, y: 4, z: 8, core: 2. Of those that a mesh axis runs over, the one named last changes fastest.
Arguments:
- tokens: bfloat16 [32768, 3072], P(('depth', 'row'), 'col')
- w_up: bfloat16 [3072, 8192], P('row', 'col')
- w_down: bfloat16 [8192, 3072], P('row', 'col')
- grad_out: bfloat16 [32768, 3072], P(('depth', 'row'), 'col')
Outputs:
- output 1: bfloat16 [32768, 3072], P(('depth', 'row'), 'col')
- output 2: bfloat16 [32768, 3072], P(('depth', 'row'), 'col')
- output 3: float32 [3072, 8192], P('row', 'col')
- output 4: float32 [8192, 3072], P('row', 'col')
All inputs are finite; a program needn't handle non-finite values.
Results may differ from a plain program's by a relative error of at most 0.00114.
Values are sent between devices in bfloat16 or wider.
A program may use at most 768 MiB of HBM per device.

v0:
```python
import jax
import jax.numpy as jnp
from jax import lax
from jax.sharding import PartitionSpec as P


def gelu_fn(pre_act):
    return jax.nn.gelu(pre_act, approximate=True)


def solution(mesh):
    act_spec = P(("depth", "row"), "col")
    weight_spec = P("row", "col")
    contract_last = (((1,), (1,)), ((), ()))
    contract_first = (((0,), (0,)), ((), ()))

    def local_block(tok_blk, up_blk, down_blk, grad_blk):
        tok_full = lax.all_gather(tok_blk, "col", axis=1, tiled=True)
        up_cols = lax.all_gather(up_blk, "row", axis=0, tiled=True)
        down_cols = lax.all_gather(down_blk, "row", axis=0, tiled=True)
        pre_act = jnp.dot(tok_full, up_cols, preferred_element_type=jnp.float32)
        hidden, gelu_vjp = jax.vjp(gelu_fn, pre_act)
        hidden = hidden.astype(jnp.bfloat16)
        hidden_full = lax.all_gather(hidden, "col", axis=1, tiled=True)
        out_blk = jnp.dot(hidden_full, down_cols, preferred_element_type=jnp.float32).astype(jnp.bfloat16)
        d_hidden_part = lax.dot_general(grad_blk, down_cols, contract_last, preferred_element_type=jnp.float32)
        d_hidden = lax.psum_scatter(d_hidden_part, "col", scatter_dimension=1, tiled=True)
        d_pre = gelu_vjp(d_hidden)[0].astype(jnp.bfloat16)
        dx_part = lax.dot_general(d_pre, up_cols, contract_last, preferred_element_type=jnp.float32)
        dx_blk = lax.psum_scatter(dx_part, "col", scatter_dimension=1, tiled=True).astype(jnp.bfloat16)
        dw_up_part = lax.dot_general(tok_full, d_pre, contract_first, preferred_element_type=jnp.float32)
        dw_up_layer = lax.psum_scatter(dw_up_part, "row", scatter_dimension=0, tiled=True)
        dw_up = lax.psum(dw_up_layer, "depth")
        dw_down_part = lax.dot_general(hidden_full, grad_blk, contract_first, preferred_element_type=jnp.float32)
        dw_down_layer = lax.psum_scatter(dw_down_part, "row", scatter_dimension=0, tiled=True)
        dw_down = lax.psum(dw_down_layer, "depth")
        return out_blk, dx_blk, dw_up, dw_down

    return jax.shard_map(local_block, mesh=mesh, in_specs=(act_spec, weight_spec, weight_spec, act_spec), out_specs=(act_spec, act_spec, weight_spec, weight_spec), check_vma=False)
```

profile of v0, /device:TPU:32, one launch (start us, length us, event | category | flops | bytes accessed | tf_op | source)
XLA Modules:
  0.0 959.4 jit_solution(10238041313338590880)
XLA Ops:
  7.2 0.0 all-gather.11.cloned.1.call-start
  7.2 0.7 all-gather.11.cloned.1.call-update
  7.9 0.0 all-gather.5.cloned.1.call-start
  8.0 0.7 all-gather.5.cloned.1.call-update
  8.7 0.0 all-gather.7.cloned.1.call-start
  8.7 0.7 all-gather.7.cloned.1.call-update
  9.4 0.0 reduce-scatter.5.cloned.1.call-start
  9.4 72.8 %all-gather.11.cloned.1.call-done = bf16[8192,768]{1,0:T(8,128)(2,1)} async-done(((bf16[1024,768]{1,0:T(8,128)(2,1)}), bf16[8192,768]{1,0:T(8,128)(2,1)}) %all-gather.11.cloned.1.call-update) | async-done | bytes 12582928 | tf_op jit(solution)/shard_map/all_gather | solution.py:20
  82.3 14.7 %fusion.7 = f32[512,8192]{1,0:T(8,128)} fusion(bf16[512,768]{1,0:T(8,128)(2,1)S(1)} %copy-done, bf16[8192,768]{1,0:T(8,128)(2,1)} %all-gather.11.cloned.1.call-done), kind=kOutput, calls=%fused_computation.12 | convolution fusion | flops 6442450944 | bytes 30146560 | tf_op jit(solution)/shard_map/dot_general | solution.py:26
  97.0 0.0 reduce-scatter.5.cloned.1.call-update
  97.1 0.0 all-gather.9.cloned.1.call-start
  97.1 29.3 %all-gather.5.cloned.1.call-done = bf16[512,3072]{1,0:T(8,128)(2,1)} async-done(((bf16[512,768]{1,0:T(8,128)(2,1)}), bf16[512,3072]{1,0:T(8,128)(2,1)}) %all-gather.5.cloned.1.call-update) | async-done | bytes 3145744 | tf_op jit(solution)/shard_map/all_gather | solution.py:18
  126.4 72.0 %all-gather.7.cloned.1.call-done = bf16[3072,2048]{1,0:T(8,128)(2,1)} async-done(((bf16[384,2048]{1,0:T(8,128)(2,1)}), bf16[3072,2048]{1,0:T(8,128)(2,1)}) %all-gather.7.cloned.1.call-update) | async-done | bytes 12582928 | tf_op jit(solution)/shard_map/all_gather | solution.py:19
  198.4 153.5 %reduce-scatter.5.cloned.1.call-done = f32[512,2048]{1,0:T(8,128)} async-done(((f32[512,8192]{1,0:T(8,128)}), f32[512,2048]{1,0:T(8,128)}) %reduce-scatter.5.cloned.1.call-update) | async-done | bytes 4194320 | tf_op jit(solution)/shard_map/reduce_scatter | solution.py:27
  351.9 16.3 %fusion.6 = (bf16[512,2048]{1,0:T(8,128)(2,1)S(1)}, bf16[512,2048]{1,0:T(8,128)(2,1)}) fusion(f32[512,2048]{1,0:T(8,128)} %reduce-scatter.5.cloned.1.call-done, bf16[512,3072]{1,0:T(8,128)(2,1)} %all-gather.5.cloned.1.call-done, bf16[3072,2048]{1,0:T(8,128)(2,1)} %all-gather.7.cloned.1.call-done), kind=kOutput, calls=%fused_computation.9 | convolution fusion | flops 6465519616 | bytes 24117248 | tf_op jit(solution)/shard_map/dot_general | solution.py:21
  368.2 0.0 all-gather.9.cloned.1.call-update
  368.2 0.0 reduce-scatter.9.cloned.1.call-start
  368.3 13.6 %convolution_bitcast_fusion = f32[3072,2048]{0,1:T(8,128)} fusion(bf16[512,2048]{1,0:T(8,128)(2,1)S(1)} %get-tuple-element.10, bf16[512,3072]{1,0:T(8,128)(2,1)} %all-gather.5.cloned.1.call-done), kind=kOutput, calls=%fused_computation | convolution fusion | flops 6442450944 | bytes 30408704 | tf_op jit(solution)/shard_map/dot_general | solution.py:31
  381.9 0.2 reduce-scatter.11.cloned.1.call-start
  382.1 71.9 %all-gather.9.cloned.1.call-done = bf16[512,8192]{1,0:T(8,128)(2,1)} async-done(((bf16[512,2048]{1,0:T(8,128)(2,1)}), bf16[512,8192]{1,0:T(8,128)(2,1)}) %all-gather.9.cloned.1.call-update) | async-done | bytes 8388624 | tf_op jit(solution)/shard_map/all_gather | solution.py:24
  454.0 14.9 %fusion.9 = f32[8192,768]{1,0:T(8,128)} fusion(bf16[512,8192]{1,0:T(8,128)(2,1)} %all-gather.9.cloned.1.call-done, bf16[512,768]{1,0:T(8,128)(2,1)S(1)} %copy-done), kind=kOutput, calls=%fused_computation.14 | convolution fusion | flops 6442450944 | bytes 34340864 | tf_op jit(solution)/shard_map/dot_general | solution.py:34
  468.9 0.0 reduce-scatter.7.cloned.1.call-start
  469.0 11.4 %fusion.8 = f32[512,3072]{1,0:T(8,128)} fusion(bf16[512,2048]{1,0:T(8,128)(2,1)S(1)} %get-tuple-element.10, bf16[3072,2048]{1,0:T(8,128)(2,1)} %all-gather.7.cloned.1.call-done), kind=kOutput, calls=%fused_computation.13 | convolution fusion | flops 6442450944 | bytes 20971520 | tf_op jit(solution)/shard_map/dot_general | solution.py:29
  480.4 0.0 all-reduce.3.cloned.1.call-start
  480.4 110.9 %reduce-scatter.9.cloned.1.call-done = f32[384,2048]{0,1:T(8,128)} async-done(((f32[3072,2048]{0,1:T(8,128)}), f32[384,2048]{0,1:T(8,128)}) %reduce-scatter.9.cloned.1.call-update) | async-done | bytes 3145744 | tf_op jit(solution)/shard_map/reduce_scatter | solution.py:32
  591.4 136.3 %reduce-scatter.11.cloned.1.call-done = f32[1024,768]{1,0:T(8,128)} async-done(((f32[8192,768]{1,0:T(8,128)}), f32[1024,768]{1,0:T(8,128)}) %reduce-scatter.11.cloned.1.call-update) | async-done | bytes 3145744 | tf_op jit(solution)/shard_map/reduce_scatter | solution.py:35
  727.7 68.9 %reduce-scatter.7.cloned.1.call-done = f32[512,768]{1,0:T(8,128)} async-done(((f32[512,3072]{1,0:T(8,128)}), f32[512,768]{1,0:T(8,128)}) %reduce-scatter.7.cloned.1.call-update) | async-done | bytes 1572880 | tf_op jit(solution)/shard_map/reduce_scatter | solution.py:30
  796.6 2.4 convert_element_type.15
  799.0 13.4 %convolution_convert_fusion = bf16[512,768]{1,0:T(8,128)(2,1)} fusion(bf16[512,8192]{1,0:T(8,128)(2,1)} %all-gather.9.cloned.1.call-done, bf16[8192,768]{1,0:T(8,128)(2,1)} %all-gather.11.cloned.1.call-done), kind=kOutput, calls=%fused_computation.11 | convolution fusion | flops 6442844160 | bytes 21757952 | tf_op jit(solution)/shard_map/dot_general | solution.py:25
  812.4 133.1 %all-reduce.3.cloned.1.call-done = (f32[384,2048]{0,1:T(8,128)}, f32[1024,768]{1,0:T(8,128)}) async-done(((f32[384,2048]{0,1:T(8,128)}, f32[1024,768]{1,0:T(8,128)}), (f32[384,2048]{0,1:T(8,128)}, f32[1024,768]{1,0:T(8,128)})) %all-reduce.3.cloned.1.call-update) | async-done | bytes 6291472 | tf_op jit(solution)/shard_map/psum | solution.py:33
  945.5 3.6 copy.8
  949.1 3.8 copy.11
  (8 shorter events, 0.1 us)
Async XLA Ops:
  7.2 75.1 %copy-start = (bf16[512,768]{1,0:T(8,128)(2,1)S(1)}, bf16[512,768]{1,0:T(8,128)(2,1)}, u32[]{:S(2)}) copy-start(bf16[512,768]{1,0:T(8,128)(2,1)} %param.7) | copy-start | bytes 2359300
  7.2 75.1 %all-gather.11.cloned.1.call-start = ((), (), s32[]{:S(2)}) async-start(), calls=%async_computation.7 | async-start | bytes 14155776 | tf_op jit(solution)/shard_map/all_gather | solution.py:20
  7.9 118.5 %all-gather.5.cloned.1.call-start = ((), (), s32[]{:S(2)}) async-start(), calls=%async_computation.4 | async-start | bytes 3932160 | tf_op jit(solution)/shard_map/all_gather | solution.py:18
  8.7 189.7 %all-gather.7.cloned.1.call-start = ((), (), s32[]{:S(2)}) async-start(), calls=%async_computation.5 | async-start | bytes 14155776 | tf_op jit(solution)/shard_map/all_gather | solution.py:19
  9.4 342.5 %reduce-scatter.5.cloned.1.call-start = ((), (), s32[]{:S(2)}) async-start(), calls=%async_computation.8 | async-start | bytes 20971520 | tf_op jit(solution)/shard_map/reduce_scatter | solution.py:27
  97.1 356.9 %all-gather.9.cloned.1.call-start = ((), (), s32[]{:S(2)}) async-start(), calls=%async_computation.6 | async-start | bytes 10485760 | tf_op jit(solution)/shard_map/all_gather | solution.py:24
  368.2 223.1 %reduce-scatter.9.cloned.1.call-start = ((), (), s32[]{:S(2)}) async-start(), calls=%async_computation.10 | async-start | bytes 28311552 | tf_op jit(solution)/shard_map/reduce_scatter | solution.py:32
  381.9 345.8 %reduce-scatter.11.cloned.1.call-start = ((), (), s32[]{:S(2)}) async-start(), calls=%async_computation.11 | async-start | bytes 28311552 | tf_op jit(solution)/shard_map/reduce_scatter | solution.py:35
  468.9 327.7 %reduce-scatter.7.cloned.1.call-start = ((), (), s32[]{:S(2)}) async-start(), calls=%async_computation.9 | async-start | bytes 7864320 | tf_op jit(solution)/shard_map/reduce_scatter | solution.py:30
  480.4 465.1 %all-reduce.3.cloned.1.call-start = ((), (), s32[]{:S(2)}) async-start(), calls=%async_computation.12 | async-start | bytes 12582912 | tf_op jit(solution)/shard_map/psum | solution.py:33
  945.5 7.4 copy-start.1
Sparse Core Ops, SparseCore 0:
  9.8 72.4 all-gather.10
  84.1 42.2 all-gather.4
  128.2 70.1 all-gather.6
  200.9 150.9 reduce-scatter.4
  368.3 85.6 all-gather.8
  456.5 134.8 reduce-scatter.8
  594.0 133.6 reduce-scatter.10
  730.2 66.2 reduce-scatter.6
  799.0 146.3 all-reduce.2
where the time goes:
time: 962 us; the launch traced here: 959 us
  waiting for transfers between devices  851 us (88%)
  matrix products  84.4 us (9%)
  between operations  13.9 us (1%)
    reduce_scatter x1, waiting for transfers between devices, local_block(): lax.psum_scatter(d_hidden_part, 'col', scatter_dimension=1, tiled=True)  153 us
    reduce_scatter x1, waiting for transfers between devices, local_block(): lax.psum_scatter(dw_down_part, 'row', scatter_dimension=0, tiled=True)  136 us
    psum x1, waiting for transfers between devices, local_block(): dw_up = lax.psum(dw_up_layer, 'depth')  133 us
    reduce_scatter x1, waiting for transfers between devices, local_block(): lax.psum_scatter(dw_up_part, 'row', scatter_dimension=0, tiled=True)  111 us
    all_gather x1, waiting for transfers between devices, local_block(): down_cols = lax.all_gather(down_blk, 'row', axis=0, tiled=True)  72.8 us
    all_gather x1, waiting for transfers between devices, local_block(): up_cols = lax.all_gather(up_blk, 'row', axis=0, tiled=True)  72 us
    all_gather x1, waiting for transfers between devices, local_block(): hidden_full = lax.all_gather(hidden, 'col', axis=1, tiled=True)  71.9 us
    reduce_scatter x1, waiting for transfers between devices, local_block(): lax.psum_scatter(dx_part, 'col', scatter_dimension=1, tiled=True)  68.9 us
  transfers between devices with their start and end apart: 9, of which 9 were waited for; matrix products, arithmetic and copies ran while one was open for 7% of the time, Pallas kernels for 0%

commit v1 on v0

v1 whole, which is shorter than its diff:
```python
import functools
import itertools

import jax
import jax.numpy as jnp
from jax import lax
from jax.experimental import pallas as pl
from jax.experimental.pallas import tpu as pltpu
from jax.sharding import PartitionSpec as P

MESH = pl.DeviceIdType.MESH
ANY = pl.BlockSpec(memory_space=pl.ANY)
F32 = jnp.float32
BF16 = jnp.bfloat16

CHUNKS_UP = [(0, 0, 1), (1, 3, 1), (0, 1, 1), (1, 4, 1), (0, 2, 1), (1, 5, 1)]
CHUNKS_DOWN_X = [(0, 0, 2), (1, 4, 2), (0, 2, 2), (1, 6, 2)]
CHUNKS_DOWN_Z = [(0, 8, 2), (1, 12, 2), (0, 10, 2), (1, 14, 2)]


def gelu_fn(pre_act):
    return jax.nn.gelu(pre_act, approximate=True)


class Plan:
    def __init__(self, rates, window):
        self.rates, self.window = rates, window
        self.tasks, self.size, self.link = [], {}, {}

    def msg(self, key, link, nbytes):
        self.size[key], self.link[key] = nbytes, link

    def task(self, prio, waits, sends, run, cost=0.3, stage=None):
        self.tasks.append((prio, tuple(waits), tuple(sends), run, cost, stage))

    def order(self):
        free, arrive, out = {}, {}, []
        now, left = 0.0, list(range(len(self.tasks)))
        while left:
            best = None
            for i in left:
                prio, waits, sends, _, _, _ = self.tasks[i]
                if any(w not in arrive for w in waits):
                    continue
                ready = max([arrive[w] for w in waits], default=0.0)
                if not waits:
                    ready = max([free.get(self.link[s], 0.0) - self.window for s in sends], default=0.0)
                key = (max(ready, now), prio, i)
                if best is None or key < best:
                    best = key
            at, _, i = best
            left.remove(i)
            out.append(i)
            now = at + self.tasks[i][4]
            for s in self.tasks[i][2]:
                rate, lat = self.rates[self.link[s][0]]
                done = max(now, free.get(self.link[s], 0.0)) + self.size[s] / rate
                free[self.link[s]] = done
                arrive[s] = done + lat
        self.end = max(now, max(arrive.values()))
        return out


RATES = {"x": (44e3, 2.5), "y": (44e3, 2.5), "z": (44e3, 2.5), "d": (300e3, 1.5), "t": (40e3, 5.0), "l": (1e12, 0.0)}
WINDOW = 8.0


class Comm:
    def __init__(self, plan, ssem, rsem):
        self.plan, self.ssem, self.rsem = plan, ssem, rsem
        self.make, self.slot, self.remote_if = {}, {}, {}

    def msg(self, key, link, src, dst, to):
        i = len(self.slot)
        self.slot[key] = i
        self.make[key] = lambda: pltpu.make_async_remote_copy(
            src_ref=src(), dst_ref=dst(), send_sem=self.ssem.at[i], recv_sem=self.rsem.at[i], device_id=to, device_id_type=MESH)
        shape = src().shape
        nbytes = functools.reduce(lambda a, b: a * b, shape, 1) * src().dtype.itemsize
        self.plan.msg(key, link, nbytes)

    def each(self, keys, act):
        for key in keys:
            if key not in self.make:
                continue
            if key in self.remote_if:
                pl.when(self.remote_if[key])(lambda key=key: act(self.make[key]()))
            else:
                act(self.make[key]())

    def start(self, *keys):
        self.each(keys, lambda copy: copy.start())

    def wait(self, *keys):
        self.each(keys, lambda copy: copy.wait_recv())

    def finish(self):
        self.each(list(self.make), lambda copy: copy.wait_send())


def where_am_i():
    z, y, r = lax.axis_index("depth"), lax.axis_index("col"), lax.axis_index("row")
    return z, y, lax.div(r, 2), lax.rem(r, 2)


def gather_kernel(dims, x_ref, g_ref, w1_ref, w2_ref, xf, gf, w1c, w2c, vx, vg, vw1, vw2, lsem, ssem, rsem):
    nz, ny, nx = dims
    z, y, x, c = where_am_i()
    tk, hb = x_ref.shape
    fc = w2_ref.shape[0]
    hr = hb // 2
    fz = fc // nz
    r = 2 * x + c

    def col(d):
        return {"col": lax.rem(y + d + ny, ny)}

    def row(d):
        return {"row": 2 * lax.rem(x + d + nx, nx) + c}

    def dep(d):
        return {"depth": lax.rem(z + d + nz, nz)}

    partner = {"row": 2 * x + (1 - c)}

    def target(t):
        return {"row": 2 * lax.rem(x + t, nx) + c, "col": x}

    loads = [
        pltpu.make_async_copy(w2_ref.at[pl.ds(z * fz, fz), :], vw2, lsem.at[0]),
        pltpu.make_async_copy(w1_ref, vw1, lsem.at[1]),
        pltpu.make_async_copy(x_ref, vx, lsem.at[2]),
        pltpu.make_async_copy(g_ref, vg, lsem.at[3]),
    ]
    for copy in loads:
        copy.start()

    barrier = pltpu.get_barrier_semaphore()

    def tell(to):
        pl.semaphore_signal(barrier, inc=1, device_id=to, device_id_type=MESH)

    for to in (col(1), col(-1), row(1), row(-1), dep(1), dep(-1), partner):
        tell(to)
    for b in range(1, ny):
        tell({"row": 2 * y + c, "col": lax.rem(y + b, ny)})

    @pl.when(x != y)
    def _():
        tell({"row": 2 * y + c, "col": y})

    pl.semaphore_wait(barrier, 10 + jnp.where(x != y, 1, 0))

    def xblock(full, k, lo, n):
        return full.at[pl.ds(c * tk + lo, n), pl.ds(pl.multiple_of(k * hb, hb), hb)]

    def wblock(k):
        return w1c.at[pl.ds(k * hr, hr), :]

    def wpiece(k, b):
        return w2c.at[pl.ds(k * fz, fz), pl.ds(pl.multiple_of(b * hb, hb), hb)]

    ym, yp, yo = lax.rem(y + ny - 1, ny), lax.rem(y + 1, ny), lax.rem(y + 2, ny)
    half = tk // 2
    started = []

    def send(i, src, dst, to):
        copy = pltpu.make_async_remote_copy(src_ref=src, dst_ref=dst, send_sem=ssem.at[i], recv_sem=rsem.at[i], device_id=to, device_id_type=MESH)
        copy.start()
        started.append(copy)

    def got(i, dst):
        pltpu.make_async_remote_copy(src_ref=dst, dst_ref=dst, send_sem=ssem.at[i], recv_sem=rsem.at[i], device_id=partner, device_id_type=MESH).wait_recv()

    def slice_copy(t):
        return pltpu.make_async_remote_copy(src_ref=vw2, dst_ref=wpiece(z, y), send_sem=ssem.at[t], recv_sem=rsem.at[y], device_id=target(t), device_id_type=MESH)

    loads[0].wait()
    for t in (1, 3, 2):
        slice_copy(t).start()

    @pl.when(x != y)
    def _():
        slice_copy(0).start()

    self_copy = pltpu.make_async_copy(vw2, wpiece(z, y), lsem.at[4])

    @pl.when(x == y)
    def _():
        self_copy.start()

    c0 = pl.multiple_of(c * fc, fc)
    c1 = pl.multiple_of((1 - c) * fc, fc)
    loads[1].wait()
    send(36, vw1.at[:, pl.ds(c1, fc)], wblock(r), partner)
    for i, d in ((37, 1), (38, -1)):
        send(i, vw1.at[:, pl.ds(c0, fc)], wblock(r), row(d))
    keep = [pltpu.make_async_copy(vw1.at[:, pl.ds(c0, fc)], wblock(r), lsem.at[5])]
    loads[2].wait()
    loads[3].wait()
    base = {0: 44, 1: 53}
    for a, (v, full) in enumerate(((vx, xf), (vg, gf))):
        send(base[a], v, xblock(full, y, 0, tk), col(1))
        send(base[a] + 1, v, xblock(full, y, 0, tk), col(-1))
    for a, (v, full) in enumerate(((vx, xf), (vg, gf))):
        send(base[a] + 4, v, xblock(full, y, 0, tk), partner)
        keep.append(pltpu.make_async_copy(v, xblock(full, y, 0, tk), lsem.at[6 + a]))
    for copy in keep:
        copy.start()

    rp = 2 * x + 1 - c
    got(36, wblock(rp))
    for i, d in ((39, 1), (40, -1)):
        send(i, wblock(rp), wblock(rp), row(d))

    def z_index(o, step, sign):
        return 4 + o * 8 + (step if sign > 0 else 4 + step)

    def z_send(o, step, sign):
        b = lax.rem(y + o, ny)
        k = lax.rem(z - sign * step + nz, nz)
        src = wpiece(k, b)
        send(z_index(o, step, sign), src, wpiece(k, b), dep(sign))

    def z_got(o, step, sign):
        b = lax.rem(y + o, ny)
        got(z_index(o, step, sign), wpiece(lax.rem(z - sign * (step + 1) + nz, nz), b))

    def z_steps(o, sign):
        return 4 if (sign > 0) == (o % 2 == 0) else 3

    def z_first(o):
        b = lax.rem(y + o, ny)
        if o == 0:
            @pl.when(x != y)
            def _():
                got(b, wpiece(z, b))

            @pl.when(x == y)
            def _():
                self_copy.wait()
        else:
            got(b, wpiece(z, b))
        for sign in (1, -1):
            z_send(o, 0, sign)

    def z_forward(step):
        for o in range(ny):
            for sign in (1, -1):
                if step < z_steps(o, sign):
                    z_got(o, step, sign)
                    if step + 1 < z_steps(o, sign):
                        z_send(o, step + 1, sign)

    def x_arrived(a, full):
        got(base[a], xblock(full, ym, 0, tk))
        send(base[a] + 2, xblock(full, ym, 0, half), xblock(full, ym, 0, half), col(1))
        got(base[a] + 1, xblock(full, yp, 0, tk))
        send(base[a] + 3, xblock(full, yp, half, half), xblock(full, yp, half, half), col(-1))
        send(base[a] + 5, xblock(full, ym, 0, tk), xblock(full, ym, 0, tk), partner)
        send(base[a] + 6, xblock(full, yp, 0, tk), xblock(full, yp, 0, tk), partner)

    def x_opposite(a, full):
        got(base[a] + 2, xblock(full, yo, 0, half))
        send(base[a] + 7, xblock(full, yo, 0, half), xblock(full, yo, 0, half), partner)
        got(base[a] + 3, xblock(full, yo, half, half))
        send(base[a] + 8, xblock(full, yo, half, half), xblock(full, yo, half, half), partner)

    z_first(0)
    z_first(1)
    z_first(3)
    z_first(2)
    x_arrived(0, xf)
    z_forward(0)
    xm, xp = lax.rem(x + nx - 1, nx), lax.rem(x + 1, nx)
    xo = lax.rem(x + 2, nx)
    got(37, wblock(2 * xm + c))
    send(41, wblock(2 * xm + c), wblock(2 * xm + c), row(1))
    got(38, wblock(2 * xp + c))
    x_arrived(1, gf)
    z_forward(1)
    x_opposite(0, xf)
    got(39, wblock(2 * xm + 1 - c))
    got(40, wblock(2 * xp + 1 - c))
    send(42, wblock(2 * xp + 1 - c), wblock(2 * xp + 1 - c), row(-1))
    z_forward(2)
    x_opposite(1, gf)
    got(41, wblock(2 * xo + c))
    got(42, wblock(2 * xo + 1 - c))
    z_forward(3)

    pc = 1 - c
    for a, full in ((0, xf), (1, gf)):
        def pblock(k, lo, n):
            return full.at[pl.ds(pc * tk + lo, n), pl.ds(pl.multiple_of(k * hb, hb), hb)]
        got(base[a] + 4, pblock(y, 0, tk))
        got(base[a] + 5, pblock(ym, 0, tk))
        got(base[a] + 6, pblock(yp, 0, tk))
        got(base[a] + 7, pblock(yo, 0, half))
        got(base[a] + 8, pblock(yo, half, half))
    for copy in keep:
        copy.wait()
    for copy in started:
        copy.wait_send()
    for t in (1, 3, 2):
        slice_copy(t).wait_send()

    @pl.when(x != y)
    def _():
        slice_copy(0).wait_send()


def gather(dims, tok, grad, up, down):
    tk, hb = tok.shape
    fc = down.shape[0]
    nz, ny, nx = dims
    return pl.pallas_call(
        functools.partial(gather_kernel, dims),
        out_shape=[
            jax.ShapeDtypeStruct((2 * tk, ny * hb), BF16),
            jax.ShapeDtypeStruct((2 * tk, ny * hb), BF16),
            jax.ShapeDtypeStruct((nx * hb, fc), BF16),
            jax.ShapeDtypeStruct((fc, ny * hb), BF16),
        ],
        in_specs=[ANY] * 4,
        out_specs=[ANY] * 4,
        scratch_shapes=[
            pltpu.VMEM((tk, hb), BF16),
            pltpu.VMEM((tk, hb), BF16),
            pltpu.VMEM(up.shape, BF16),
            pltpu.VMEM((fc // nz, hb), BF16),
            pltpu.SemaphoreType.DMA((8,)),
            pltpu.SemaphoreType.DMA((64,)),
            pltpu.SemaphoreType.DMA((64,)),
        ],
        compiler_params=pltpu.CompilerParams(collective_id=0, has_side_effects=True),
        name="gather",
    )(tok, grad, up, down)


def each(shape, fn):
    lead = shape[:-2]
    big = max(range(len(lead)), key=lambda d: lead[d])
    looped = lead[big] >= 8

    def rest(k):
        for ix in itertools.product(*[range(n) if not (looped and d == big) else (k,) for d, n in enumerate(lead)]):
            fn(ix)

    if looped:
        pl.loop(0, lead[big])(rest)
    else:
        rest(None)


def accumulate(dst, others):
    def one(ix):
        total = dst[ix]
        for o in others:
            total = total + o[ix]
        dst[ix] = total

    each(dst.shape, one)


def reduce_kernel(dims, yp, dxp, dw1, dw2, y_out, dx_out, dw1_out, dw2_out, *scratch):
    nz, ny, nx = dims
    z, y, x, c = where_am_i()
    fc = dw1.shape[-1]
    hb = y_out.shape[-1]
    sgn = (1, -1)
    scratch = list(scratch)

    def grab(n):
        return [scratch.pop(0) for _ in range(n)]

    n1, n2, n3 = len(CHUNKS_UP), len(CHUNKS_DOWN_X), len(CHUNKS_DOWN_Z)
    ux, uz, us = grab(n1), grab(n1), grab(n1)
    vx, vz, vt = grab(n2), grab(n2), grab(n2)
    wz, wx, wt = grab(n3), grab(n3), grab(n3)
    o1, o2, pair, yr, yo = grab(5)
    pools = grab(4)
    ssem, rsem, lsem, osem = grab(4)

    plan = Plan(RATES, WINDOW)
    comm = Comm(plan, ssem, rsem)

    def idx(axis, d):
        at, n = {"z": (z, nz), "y": (y, ny), "x": (x, nx)}[axis]
        return lax.rem(at + (d % n), n)

    def nb(axis, d):
        i = idx(axis, d)
        return {"z": {"depth": i}, "y": {"col": i}, "x": {"row": 2 * i + c}}[axis]

    partner = {"row": 2 * x + (1 - c)}
    across = {"row": 2 * y + c, "col": x}

    def hcol(j):
        return pl.ds(pl.multiple_of(j * hb, hb), hb)

    def fcol(h):
        return pl.ds(pl.multiple_of(h * fc, fc), fc)

    staged, stores = [], []

    def stage(pool, src):
        staged.append((pool, src))
        return len(staged) - 1

    def mark(key):
        plan.msg(key, ("l", key), 0)

    place = {}

    def slot(k):
        return place[k][0]

    def chain(key, axis, n, s, buf, src, pool, prio, end, end_sends, end_waits=()):
        far, near = n // 2, n // 2 - 1
        for t in range(far):
            comm.msg((key, "F", t), (axis, s), (lambda: src(far * s)) if t == 0 else (lambda t=t: buf.at[t - 1]), lambda t=t: buf.at[t], nb(axis, s))
        for t in range(near):
            comm.msg((key, "N", t), (axis, -s), (lambda: src(-near * s)) if t == 0 else (lambda t=t: buf.at[far + t - 1]), lambda t=t: buf.at[far + t], nb(axis, -s))

        def mid(name, t, at, rel, extra):
            k = None if pool is None else stage(pool, lambda: src(rel))

            def run():
                accumulate(buf.at[at], [src(rel) if k is None else slot(k)])
                comm.start((key, name, t + 1))

            plan.task(prio, [(key, name, t), *extra], [(key, name, t + 1)], run, stage=k)

        for t in range(far - 1):
            mid("F", t, t, (far - 1 - t) * s, end_waits[1:2] if end_waits else ())
        for t in range(near - 1):
            mid("N", t, far + t, -(near - 1 - t) * s, ())
        k = None if pool is None else stage(pool, lambda: src(0))
        last = [buf.at[far - 1], buf.at[far + near - 1]]
        plan.task(prio, [(key, "F", far - 1), (key, "N", near - 1), *end_waits[:1]], end_sends,
                  lambda: end(last, src(0) if k is None else slot(k)), stage=k)
        return [(key, "F", 0), (key, "N", 0)]

    def spread(key, s, region, store):
        far, near = nz // 2, nz // 2 - 1
        for name, count, d in (("GF", far, s), ("GN", near, -s)):
            for t in range(count):
                def ref(t=t, d=d):
                    return region(idx("z", -t * d))
                comm.msg((key, name, t), ("z", d), ref, ref, nb("z", d))
        for name, count in (("GF", far), ("GN", near)):
            for t in range(count - 1):
                plan.task(4, [(key, name, t)], [(key, name, t + 1)], lambda name=name, t=t: comm.start((key, name, t + 1)), 0.15)
        plan.task(30, [(key, "GF", far - 1), (key, "GN", near - 1)], [], store, 0.15)
        return [(key, "GF", 0), (key, "GN", 0)]

    def store(src, dst):
        copy = pltpu.make_async_copy(src, dst, osem.at[len(stores)])
        stores.append(copy)
        copy.start()

    for i, (sigma, q, n) in enumerate(CHUNKS_UP):
        s = sgn[sigma]
        res = ux[i].at[1]

        def region(k, q=q, n=n):
            return o1.at[k, pl.ds(q, n)]

        first = spread(("ug", i), s, region, lambda q=q, n=n: store(o1.at[:, pl.ds(q, n)], dw1_out.at[:, pl.ds(q, n)]))
        comm.msg(("sw", i), ("d", 0), lambda i=i: us[i], lambda q=q, n=n: o1.at[z, pl.ds(q, n), :, fcol(c)], partner)
        plan.task(3, [("sw", i)], first, lambda first=first: comm.start(*first))

        def z_end(last, own, i=i, q=q, n=n):
            for m in range(n):
                o1[z, q + m, :, fcol(c)] = own[c, m] + last[0][c, m] + last[1][c, m]
                us[i][m] = own[1 - c, m] + last[0][1 - c, m] + last[1][1 - c, m]
            comm.start(("sw", i))

        raws = chain(("uz", i), "z", nz, s, uz[i], lambda rel, res=res: res.at[:, idx("z", rel)], None, 5, z_end, [("sw", i)])

        def x_end(last, own, raws=raws):
            accumulate(last[0], [last[1], own])
            comm.start(*raws)

        raws = chain(("ux", i), "x", nx, s, ux[i], lambda rel, q=q, n=n: dw1.at[idx("x", rel), :, :, pl.ds(q, n)], 0, 10, x_end, raws)
        plan.task(20 + i, [], raws, lambda raws=raws: comm.start(*raws))

    def deliver(key, i, s, u, n, tb):
        def region(k):
            return o2.at[k, pl.ds(u, n)]

        first = spread((key, "g", i), s, region, lambda: store(o2.at[:, pl.ds(u, n)], dw2_out.at[:, pl.ds(u, n)]))
        tr = (key, "tr", i)
        comm.msg(tr, ("t", 0), lambda: tb, lambda: region(z), across)
        comm.remote_if[tr] = x != y
        plan.task(3, [tr], first, lambda: comm.start(*first))

        def end(last, own):
            for m in range(n):
                tb[m] = own[m] + last[0][m] + last[1][m]
            comm.start(tr)

            @pl.when(x == y)
            def _():
                for m in range(n):
                    o2[z, u + m] = tb[m]

        return end, [tr]

    for i, (sigma, u, n) in enumerate(CHUNKS_DOWN_X):
        s = sgn[sigma]
        res = vx[i].at[1]
        end, sends = deliver("v", i, s, u, n, vt[i])
        raws = chain(("vz", i), "z", nz, s, vz[i], lambda rel, res=res: res.at[idx("z", rel)], None, 5, end, sends)

        def x_end(last, own, raws=raws):
            accumulate(last[0], [last[1], own])
            comm.start(*raws)

        raws = chain(("vx", i), "x", nx, s, vx[i], lambda rel, u=u, n=n: dw2.at[:, pl.ds(u, n), :, hcol(idx("x", rel))], 1, 10, x_end, raws)
        plan.task(20 + n1 + i, [], raws, lambda raws=raws: comm.start(*raws))

    for i, (sigma, u, n) in enumerate(CHUNKS_DOWN_Z):
        s = sgn[sigma]
        res = wz[i].at[nz // 2 - 1]
        end, sends = deliver("w", i, s, u, n, wt[i])
        raws = chain(("wx", i), "x", nx, s, wx[i], lambda rel, res=res: res.at[:, :, hcol(idx("x", rel))], None, 8, end, sends)

        def z_end(last, own, raws=raws):
            accumulate(last[0], [last[1], own])
            comm.start(*raws)

        raws = chain(("wz", i), "z", nz, s, wz[i], lambda rel, u=u, n=n: dw2.at[idx("z", rel), pl.ds(u, n)], 2, 9, z_end, raws)
        plan.task(20 + i, [], raws, lambda raws=raws: comm.start(*raws))

    rows = yo.shape[1] // 2
    for a, (part, out) in enumerate(((yp, y_out), (dxp, dx_out))):
        raw_of = {2: [], 3: [], 1: [], 0: []}
        for sigma in range(2):
            s = sgn[sigma]
            half = pl.ds(sigma * rows, rows)

            def y_end(last, own, a=a, half=half, sigma=sigma, out=out):
                @pl.loop(0, rows)
                def _(k):
                    yo[a, sigma * rows + k] = (own[k] + last[0][k] + last[1][k]).astype(BF16)

                store(yo.at[a, half], out.at[half])

            raws = chain(("y", a, sigma), "y", ny, s, yr.at[a, sigma], lambda rel, a=a, half=half: pair.at[a, rel % ny, half], None, 12, y_end, [],
                         (("pd", a, 0), ("pd", a, s % ny)))
            raw_of[2].append(raws[0])
            raw_of[-s % ny].append(raws[1])
        for n, o in enumerate((2, 3, 1, 0)):
            comm.msg(("p", a, o), ("d", 0), lambda part=part, o=o: part.at[1 - c, :, :, hcol(idx("y", o))], lambda a=a, o=o: pair.at[a, o], partner)
            mark(("pd", a, o))
            plan.task(15, [], [("p", a, o)], lambda a=a, o=o: comm.start(("p", a, o)), 0.15)
            k = stage(3, lambda part=part, o=o: part.at[c, :, :, hcol(idx("y", o))])

            def combine(a=a, o=o, k=k, go=raw_of[o]):
                accumulate(pair.at[a, o], [slot(k)])
                comm.start(*go)

            plan.task(14, [("p", a, o)], [("pd", a, o), *raw_of[o]], combine, 1.0, stage=k)

    order = plan.order()

    uses = {p: [] for p in range(len(pools))}
    for i in order:
        k = plan.tasks[i][5]
        if k is not None:
            uses[staged[k][0]].append(k)
    lbase, fill = 0, {}
    for p, ks in uses.items():
        depth = pools[p].shape[0]
        for n, k in enumerate(ks):
            place[k] = (pools[p].at[n % depth], lsem.at[lbase + n % depth])
            if n + depth < len(ks):
                fill[k] = ks[n + depth]
        lbase += depth

    def load(k):
        return pltpu.make_async_copy(staged[k][1](), *place[k])

    for p, ks in uses.items():
        for k in ks[: pools[p].shape[0]]:
            load(k).start()

    barrier = pltpu.get_barrier_semaphore()

    def tell(to):
        pl.semaphore_signal(barrier, inc=1, device_id=to, device_id_type=MESH)

    for to in (*[nb(axis, d) for axis in "zyx" for d in (1, -1)], partner):
        tell(to)

    @pl.when(x != y)
    def _():
        tell(across)

    pl.semaphore_wait(barrier, 7 + jnp.where(x != y, 1, 0))

    for i in order:
        _, waits, _, run, _, k = plan.tasks[i]
        if k is not None:
            load(k).wait()
        comm.wait(*waits)
        run()
        if k in fill:
            load(fill[k]).start()
    for copy in stores:
        copy.wait()
    comm.finish()


def reduce(dims, yp, dxp, dw1, dw2):
    nz, ny, nx = dims
    fc, hh = dw2.shape
    hb = hh // ny
    tk = yp.shape[0] // 2
    t8 = tk // 8
    nq, nu = hb // (2 * nz * 8), fc // (nz * 8)
    n_msg = 2 * 0
    vm = pltpu.VMEM

    def per(chunks, shape, count):
        return [vm(((count,) if count else ()) + shape(n), F32) for _, _, n in chunks]

    scratch = [
        *per(CHUNKS_UP, lambda n: (2, nz, n, 8, fc), nx - 1),
        *per(CHUNKS_UP, lambda n: (2, n, 8, fc), nz - 1),
        *per(CHUNKS_UP, lambda n: (n, 8, fc), 0),
        *per(CHUNKS_DOWN_X, lambda n: (nz, n, 8, hb), nx - 1),
        *per(CHUNKS_DOWN_X, lambda n: (n, 8, hb), nz - 1),
        *per(CHUNKS_DOWN_X, lambda n: (n, 8, hb), 0),
        *per(CHUNKS_DOWN_Z, lambda n: (n, 8, hh), nz - 1),
        *per(CHUNKS_DOWN_Z, lambda n: (n, 8, hb), nx - 1),
        *per(CHUNKS_DOWN_Z, lambda n: (n, 8, hb), 0),
        vm((nz, nq, 8, 2 * fc), F32),
        vm((nz, nu, 8, hb), F32),
        vm((2, ny, t8, 8, hb), F32),
        vm((2, 2, ny - 1, t8 // 2, 8, hb), F32),
        vm((2, t8, 8, hb), BF16),
        vm((4, 2, nz, CHUNKS_UP[0][2], 8, fc), F32),
        vm((4, nz, CHUNKS_DOWN_X[0][2], 8, hb), F32),
        vm((6, CHUNKS_DOWN_Z[0][2], 8, hh), F32),
        vm((2, t8, 8, hb), F32),
        pltpu.SemaphoreType.DMA((320,)),
        pltpu.SemaphoreType.DMA((320,)),
        pltpu.SemaphoreType.DMA((16,)),
        pltpu.SemaphoreType.DMA((24,)),
    ]
    y, dx, g1, g2 = pl.pallas_call(
        functools.partial(reduce_kernel, dims),
        out_shape=[
            jax.ShapeDtypeStruct((t8, 8, hb), BF16),
            jax.ShapeDtypeStruct((t8, 8, hb), BF16),
            jax.ShapeDtypeStruct((nz, nq, 8, 2 * fc), F32),
            jax.ShapeDtypeStruct((nz, nu, 8, hb), F32),
        ],
        in_specs=[ANY] * 4,
        out_specs=[ANY] * 4,
        scratch_shapes=scratch,
        compiler_params=pltpu.CompilerParams(collective_id=1, has_side_effects=True, vmem_limit_bytes=66_000_000),
        name="reduce",
    )(
        yp.reshape(2, t8, 8, hh),
        dxp.reshape(2, t8, 8, hh),
        dw1.reshape(nx, 2, nz, nq, 8, fc),
        dw2.reshape(nz, nu, 8, hh),
    )
    return y.reshape(tk, hb), dx.reshape(tk, hb), g1.reshape(nz * nq * 8, 2 * fc), g2.reshape(fc, hb)


def solution(mesh):
    act_spec = P(("depth", "row"), "col")
    weight_spec = P("row", "col")
    dims = (mesh.shape["depth"], mesh.shape["col"], mesh.shape["row"] // 2)
    last = (((1,), (1,)), ((), ()))
    first = (((0,), (0,)), ((), ()))

    def local_block(tok_blk, up_blk, down_blk, grad_blk):
        tok, grad, up, down = gather(dims, tok_blk, grad_blk, up_blk, down_blk)
        pre_act = jnp.dot(tok, up, preferred_element_type=F32)
        hidden, gelu_vjp = jax.vjp(gelu_fn, pre_act)
        hidden = hidden.astype(BF16)
        d_hidden = lax.dot_general(grad, down, last, preferred_element_type=F32)
        d_pre = gelu_vjp(d_hidden)[0].astype(BF16)
        dw_down = lax.dot_general(hidden, grad, first, preferred_element_type=F32)
        dw_up = lax.dot_general(tok, d_pre, first, preferred_element_type=F32)
        out_part = jnp.dot(hidden, down, preferred_element_type=F32)
        dx_part = lax.dot_general(d_pre, up, last, preferred_element_type=F32)
        return reduce(dims, out_part, dx_part, dw_up, dw_down)

    return jax.shard_map(local_block, mesh=mesh, in_specs=(act_spec, weight_spec, weight_spec, act_spec), out_specs=(act_spec, act_spec, weight_spec, weight_spec), check_vma=False)
```

time: 962 us -> 377 us (0.39)
  waiting for transfers between devices: 851 us -> 0 us
  Pallas kernels: 0 us -> 303 us
  matrix products: 84.4 us -> 58.9 us
  between operations: 13.9 us -> 0.73 us
    reduce_scatter x4 -> x0, waiting for transfers between devices: 470 us -> none  [the longest x1 153 us: local_block(): lax.psum_scatter(d_hidden_part, 'col', scatter_dimension=1, tiled=True)]
    pallas_call x0 -> x2, Pallas kernels: none -> 303 us  [the longest x1 224 us: reduce(): pl.pallas_call(functools.partial(reduce_kernel, dims), out_shape=[jax.Sha...]
    all_gather x4 -> x0, waiting for transfers between devices: 246 us -> none  [the longest x1 72.8 us: local_block(): down_cols = lax.all_gather(down_blk, 'row', axis=0, tiled=True)]
    psum x1 -> x0, waiting for transfers between devices: 133 us -> none  [local_block(): dw_up = lax.psum(dw_up_layer, 'depth')]
    dot_general x6, matrix products: 84.4 us -> 58.9 us  [the longest x1 10.8 us: local_block(): d_hidden = lax.dot_general(grad, down, last, preferred_element_type=F32)]
  transfers between devices with their start and end apart: 9 -> 0, of which waited for: 9 -> 0; matrix products, arithmetic and copies ran while one was open for 7% -> 0% of each run, Pallas kernels for 0% -> 0%
where the time goes in v1:
time: 377 us; the launch traced here: 370 us
  Pallas kernels  303 us (80%)
  matrix products  58.9 us (16%)
  local copies, waits for them, and re-layouts  7.79 us (2%)
    pallas_call x1, Pallas kernels, reduce(): pl.pallas_call(functools.partial(reduce_kernel, dims), out_shape=[jax.Sha...  224 us
    pallas_call x1, Pallas kernels, gather(): pl.pallas_call(functools.partial(gather_kernel, dims), out_shape=[jax.Sha...  78.5 us
    dot_general x1, matrix products, local_block(): d_hidden = lax.dot_general(grad, down, last, preferred_element_type=F32)  10.8 us
    dot_general x1, matrix products, local_block(): dw_down = lax.dot_general(hidden, grad, first, preferred_element_type=F32)  10.5 us
    dot_general x1, matrix products, local_block(): out_part = jnp.dot(hidden, down, preferred_element_type=F32)  9.97 us
    dot_general x1, matrix products, local_block(): dw_up = lax.dot_general(tok, d_pre, first, preferred_element_type=F32)  9.47 us
    dot_general x1, matrix products, local_block(): dx_part = lax.dot_general(d_pre, up, last, preferred_element_type=F32)  9.26 us
    dot_general x1, matrix products, local_block(): pre_act = jnp.dot(tok, up, preferred_element_type=F32)  8.9 us

profile of v1, /device:TPU:32, one launch (start us, length us, event | category | flops | bytes accessed | tf_op | source)
XLA Modules:
  0.0 370.0 jit_solution(1321223536796668528)
XLA Ops:
  0.6 78.5 %gather.1 = (bf16[1024,3072]{1,0:T(8,128)(2,1)}, bf16[1024,3072]{1,0:T(8,128)(2,1)}, bf16[3072,1024]{1,0:T(8,128)(2,1)}, bf16[1024,3072]{1,0:T(8,128)(2,1)}) custom-call(bf16[512,768]{1,0:T(8,128)(2,1)} %x_ref.1, bf16[512,768]{1,0:T(8,128)(2,1)} %g_ref.1, bf16[384,2048]{1,0:T(8,128)(2,1)} %w1_ref.1, bf16[1024,768]{1,0:T(8,128)(2,1)} %w2_ref.1), custom_call_target="tpu_custom_call" | custom-call | tf_op jit(solution)/shard_map/gather/pallas_call | solution.py:317
  79.2 0.0 copy-start.2
  79.2 0.0 copy-start.3
  79.2 10.8 %fusion.9 = f32[1024,1024]{1,0:T(8,128)S(1)} fusion(bf16[1024,3072]{1,0:T(8,128)(2,1)} %get-tuple-element.15, bf16[1024,3072]{1,0:T(8,128)(2,1)} %get-tuple-element.14), kind=kOutput, calls=%fused_computation.12 | convolution fusion | flops 6442450944 | bytes 16777216 | tf_op jit(solution)/shard_map/dot_general | solution.py:688
  90.0 0.0 copy-done.2
  90.0 0.0 copy-done.3
  90.0 0.0 slice-start.2
  90.0 8.9 %fusion.6 = (bf16[1024,1024]{1,0:T(8,128)(2,1)S(1)}, f32[1024,1024]{1,0:T(8,128)S(1)}) fusion(f32[1024,1024]{1,0:T(8,128)S(1)} %fusion.9, bf16[1024,3072]{1,0:T(8,128)(2,1)S(1)} %copy-done.3, bf16[3072,1024]{1,0:T(8,128)(2,1)S(1)} %copy-done.2), kind=kOutput, calls=%fused_computation.8 | convolution fusion | flops 6463422464 | bytes 23068672 | tf_op jit(solution)/shard_map/dot_general | solution.py:685
  98.9 0.0 slice-start.3
  99.0 9.5 %fusion.11 = f32[3072,1024]{1,0:T(8,128)} fusion(bf16[1024,3072]{1,0:T(8,128)(2,1)S(1)} %copy-done.3, bf16[1024,1024]{1,0:T(8,128)(2,1)S(1)} %get-tuple-element.20), kind=kOutput, calls=%fused_computation.14 | convolution fusion | flops 6442450944 | bytes 20971520 | tf_op jit(solution)/shard_map/dot_general | solution.py:691
  108.4 0.0 slice-start
  108.4 9.3 %fusion.10 = f32[1024,3072]{1,0:T(8,128)} fusion(bf16[1024,1024]{1,0:T(8,128)(2,1)S(1)} %get-tuple-element.20, bf16[3072,1024]{1,0:T(8,128)(2,1)S(1)} %copy-done.2), kind=kOutput, calls=%fused_computation.13 | convolution fusion | flops 6442450944 | bytes 20971520 | tf_op jit(solution)/shard_map/dot_general | solution.py:693
  117.7 0.0 slice-done.2
  117.7 0.0 slice-done.3
  117.7 0.0 slice-start.1
  117.7 10.0 %fusion.8 = f32[1024,3072]{1,0:T(8,128)} fusion(bf16[1024,3072]{1,0:T(8,128)(2,1)S(1)} %bitcast.29, f32[1024,1024]{1,0:T(8,128)S(1)} %get-tuple-element.21), kind=kOutput, calls=%fused_computation.11 | convolution fusion | flops 6451888128 | bytes 23068672 | tf_op jit(solution)/shard_map/dot_general | solution.py:692
  127.7 0.0 slice-done
  127.7 0.0 slice-done.1
  127.7 10.5 %fusion.7 = f32[1024,3072]{1,0:T(8,128)} fusion(bf16[1024,3072]{1,0:T(8,128)(2,1)S(1)} %bitcast.27, f32[1024,1024]{1,0:T(8,128)S(1)} %get-tuple-element.21), kind=kOutput, calls=%fused_computation.10 | convolution fusion | flops 6451888128 | bytes 23068672 | tf_op jit(solution)/shard_map/dot_general | solution.py:690
  138.2 224.1 %reduce.1 = (bf16[64,8,768]{2,1,0:T(8,128)(2,1)}, bf16[64,8,768]{2,1,0:T(8,128)(2,1)}, f32[8,6,8,2048]{3,2,1,0:T(8,128)}, f32[8,16,8,768]{3,2,1,0:T(8,128)}) custom-call(f32[2,64,8,3072]{3,2,1,0:T(8,128)} %bitcast.20, f32[2,64,8,3072]{3,2,1,0:T(8,128)} %bitcast.19, f32[4,2,8,6,8,1024]{5,4,3,2,1,0:T(8,128)} %bitcast.18, f32[8,16,8,3072]{3,2,1,0:T(8,128)} %bitcast.21), custom_call_target="tpu_custom_call" | custom-call | tf_op jit(solution)/shard_map/reduce/pallas_call | solution.py:654
  362.3 0.0 copy-start.1
  362.3 2.2 copy.12
  364.5 0.0 copy-start
  364.5 2.2 copy.13
  366.7 0.0 copy-done.1
  366.7 1.7 copy.14
  368.4 0.0 copy-done
  368.4 1.7 copy.15
  (2 shorter events, 0.0 us)
Async XLA Ops:
  79.2 10.8 %copy-start.2 = (bf16[3072,1024]{1,0:T(8,128)(2,1)S(1)}, bf16[3072,1024]{1,0:T(8,128)(2,1)}, u32[]{:S(2)}) copy-start(bf16[3072,1024]{1,0:T(8,128)(2,1)} %get-tuple-element.13) | copy-start | bytes 18874372
  79.2 10.8 %copy-start.3 = (bf16[1024,3072]{1,0:T(8,128)(2,1)S(1)}, bf16[1024,3072]{1,0:T(8,128)(2,1)}, u32[]{:S(2)}) copy-start(bf16[1024,3072]{1,0:T(8,128)(2,1)} %get-tuple-element.12) | copy-start | bytes 18874372
  90.0 27.7 %slice-start.2 = ((s8[6291456]{0:T(1024)(128)(4,1)}), s8[4194304]{0:T(1024)(128)(4,1)S(1)}, s32[]{:S(2)}) async-start(s8[6291456]{0:T(1024)(128)(4,1)} %bitcast.28), calls=%async_computation.2 | async-start | bytes 8388608
  98.9 18.8 %slice-start.3 = ((s8[6291456]{0:T(1024)(128)(4,1)}), s8[2097152]{0:T(1024)(128)(4,1)S(1)}, s32[]{:S(2)}) async-start(s8[6291456]{0:T(1024)(128)(4,1)} %bitcast.28), calls=%async_computation.3 | async-start | bytes 4194304
  108.4 19.3 %slice-start = ((s8[6291456]{0:T(1024)(128)(4,1)}), s8[2097152]{0:T(1024)(128)(4,1)S(1)}, s32[]{:S(2)}) async-start(s8[6291456]{0:T(1024)(128)(4,1)} %bitcast.26), calls=%async_computation | async-start | bytes 4194304
  117.7 10.0 %slice-start.1 = ((s8[6291456]{0:T(1024)(128)(4,1)}), s8[4194304]{0:T(1024)(128)(4,1)S(1)}, s32[]{:S(2)}) async-start(s8[6291456]{0:T(1024)(128)(4,1)} %bitcast.26), calls=%async_computation.1 | async-start | bytes 8388608
  362.3 4.4 %copy-start.1 = (f32[8,6,8,2048]{3,2,1,0:T(8,128)S(1)}, f32[8,6,8,2048]{3,2,1,0:T(8,128)}, u32[]{:S(2)}) copy-start(f32[8,6,8,2048]{3,2,1,0:T(8,128)} %get-tuple-element.18) | copy-start | bytes 9437188
  364.5 3.9 %copy-start = (f32[8,16,8,768]{3,2,1,0:T(8,128)S(1)}, f32[8,16,8,768]{3,2,1,0:T(8,128)}, u32[]{:S(2)}) copy-start(f32[8,16,8,768]{3,2,1,0:T(8,128)} %get-tuple-element.19) | copy-start | bytes 9437188

commit v2 on v0

v2 whole, which is shorter than its diff:
```python
import functools
import itertools

import jax
import jax.numpy as jnp
from jax import lax
from jax.experimental import pallas as pl
from jax.experimental.pallas import tpu as pltpu
from jax.sharding import PartitionSpec as P

MESH = pl.DeviceIdType.MESH
ANY = pl.BlockSpec(memory_space=pl.ANY)
F32 = jnp.float32
SUB = 8
BF16 = jnp.bfloat16

CHUNKS = [(1, "z", i % 2, 8 + 2 * i, 2, i) for i in range(4)]
CHUNKS += [(0, "z", i % 2, 12 + 2 * i, 2, 20 + i) for i in range(2)]
CHUNKS += [(1, "x", i % 2, 2 * i, 2, i) for i in range(4)]
CHUNKS += [(0, "x", i % 2, 2 * i, 2, 4 + i) for i in range(6)]
FAR_FIRST = (2, 1, 3, 0)
Y_ORDER = [(a, o) for a in range(2) for o in FAR_FIRST]


def job_list():
    def block(a, u, n, order=FAR_FIRST):
        return [("D", a, o, u, n) for o in order]

    head = block(1, 8, 4, range(4)) + block(1, 0, 4) + block(1, 12, 4, range(4))
    rest = block(1, 4, 4) + block(0, 0, 8) + block(0, 8, 4) + block(0, 12, 4, range(4))
    both = head + rest
    cut = len(both) // 2
    jobs = both[:cut]
    out = [[("Y", a, o, 0), ("Y", a, o, 1)] for a, o in Y_ORDER]
    for job, two in itertools.zip_longest(both[cut:], out):
        jobs += ([job] if job else []) + (two or [])
    return jobs


JOBS = job_list()
LHS_ORDER = (0, 1)
COST = {"D": {2: 0.75, 4: 1.15, 8: 1.57}, "Y": 1.15, "mid": 0.05, "fin": 0.1, "go": 0.03, "U": 3.05, "A3": 1.55, "A": 0.6, "act": 0.63}
SLACK = 40.0
VMEM_LIMIT = 66_500_000


def gelu_fn(pre_act):
    return jax.nn.gelu(pre_act, approximate=True)


class Plan:
    def __init__(self, rates, window):
        self.rates, self.window = rates, window
        self.tasks, self.size, self.link = [], {}, {}

    def msg(self, key, link, nbytes):
        self.size[key], self.link[key] = nbytes, link

    def task(self, prio, waits, sends, run, cost=0.3, stage=(), raw=False):
        self.tasks.append((prio, tuple(waits), tuple(sends), run, cost, tuple(stage), raw))

    def order(self):
        free, arrive, out = {}, {}, []
        self.when, self.arrive = [], arrive
        now, left = 2.5, list(range(len(self.tasks)))
        while left:
            best = None
            for i in left:
                prio, waits, sends, _, _, _, raw = self.tasks[i]
                if any(w not in arrive for w in waits):
                    continue
                ready = max([arrive[w] for w in waits], default=0.0)
                if raw:
                    ready = max([ready] + [free.get(self.link[s], 0.0) - self.window for s in sends])
                key = (max(ready, now), prio, i)
                if best is None or key < best:
                    best = key
            at, _, i = best
            left.remove(i)
            out.append(i)
            now = at + self.tasks[i][4]
            self.when.append(now)
            for s in self.tasks[i][2]:
                rate, lat = self.rates[self.link[s][0]]
                took = self.size[s] / rate
                if self.link[s][0] == "t":
                    ways = [(axis, d) for axis in "xy" for d in (1, -1)]
                    done = max(now, *[free.get(way, 0.0) for way in ways]) + took
                    for way in ways:
                        free[way] = max(now, free.get(way, 0.0)) + took / 2
                else:
                    done = max(now, free.get(self.link[s], 0.0)) + took
                    free[self.link[s]] = done
                arrive[s] = done + lat
        self.end = max(now, max(arrive.values()))
        return out


RATES = {"x": (42e3, 2.2), "y": (44e3, 2.2), "z": (45e3, 2.2), "d": (300e3, 3.0), "t": (42e3, 5.0), "l": (1e12, 0.0), "s": (1e12, 1.5)}
WINDOW = 6.0


class Comm:
    def __init__(self, plan, ssem, rsem):
        self.plan, self.ssem, self.rsem = plan, ssem, rsem
        self.make, self.meet, self.slot, self.remote_if, self.flying = {}, {}, {}, {}, []

    def msg(self, key, link, src, dst, to, mail=None):
        i = len(self.slot)
        self.slot[key] = i
        there, here = mail or (i, i)

        def make(r):
            return pltpu.make_async_remote_copy(
                src_ref=src(), dst_ref=dst(), send_sem=self.ssem.at[i], recv_sem=self.rsem.at[r], device_id=to, device_id_type=MESH)

        self.make[key] = lambda: make(there)
        self.meet[key] = lambda: make(here)
        shape = src().shape
        nbytes = functools.reduce(lambda a, b: a * b, shape, 1) * src().dtype.itemsize
        self.plan.msg(key, link, nbytes)

    def each(self, keys, make, act):
        for key in keys:
            if key in self.remote_if:
                pl.when(self.remote_if[key])(lambda key=key: act(make[key]()))
            elif key in make:
                act(make[key]())

    def start(self, *keys):
        self.flying.extend(keys)
        self.each(keys, self.make, lambda copy: copy.start())

    def wait(self, *keys):
        self.each(keys, self.meet, lambda copy: copy.wait_recv())

    def sent(self, before):
        keys = [key for key in self.flying if self.plan.arrive[key] <= before]
        self.flying = [key for key in self.flying if self.plan.arrive[key] > before]
        self.each(keys, self.make, lambda copy: copy.wait_send())


def run_tasks(plan, comm, order, load=None, fill={}):
    heard = set()
    for n, i in enumerate(order):
        _, waits, _, run, _, ks, _ = plan.tasks[i]
        with jax.named_scope(f"w{n}"):
            comm.wait(*[w for w in waits if w not in heard])
            heard.update(waits)
        with jax.named_scope(f"l{n}"):
            for k in ks:
                load(k).wait()
        with jax.named_scope(f"r{n}"):
            run()
        for k in fill.get(n, ()):
            load(k).start()
        comm.sent(plan.when[n] - SLACK)
    comm.sent(float("inf"))


def where_am_i():
    z, y, r = lax.axis_index("depth"), lax.axis_index("col"), lax.axis_index("row")
    return z, y, lax.div(r, 2), lax.rem(r, 2)


def each(shape, fn):
    lead = shape[:-2]
    big = max(range(len(lead)), key=lambda d: lead[d])
    looped = lead[big] >= 8

    def rest(k):
        for ix in itertools.product(*[range(n) if not (looped and d == big) else (k,) for d, n in enumerate(lead)]):
            fn(ix)

    if looped:
        pl.loop(0, lead[big])(rest)
    else:
        rest(None)


def accumulate(dst, others):
    def one(ix):
        total = dst[ix]
        for o in others:
            total = total + o[ix]
        dst[ix] = total

    each(dst.shape, one)


def mm(a, b):
    return jnp.dot(a, b, preferred_element_type=F32)


def mm_l(a, b):
    return lax.dot_general(a, b, (((0,), (0,)), ((), ())), preferred_element_type=F32)


def mm_t(a, b):
    return lax.dot_general(a, b, (((1,), (1,)), ((), ())), preferred_element_type=F32)


def gather_kernel(dims, x_ref, g_ref, w1_ref, w2_ref, xf, gf, w1f, w2f, hid, dpre,
                  bx, bg, bw1, bw2, vw2, u, da, ha, hd, ssem, rsem, lsem, osem):
    nz, ny, nx = dims
    z, y, x, c = where_am_i()
    tk, hb = x_ref.shape
    fc = w2_ref.shape[0]
    hr, fz, half = hb // 2, fc // nz, tk // 2
    plan = Plan(RATES, WINDOW)
    comm = Comm(plan, ssem, rsem)
    ways = (1, -1)

    def idx(axis, d):
        at, n = {"z": (z, nz), "y": (y, ny), "x": (x, nx)}[axis]
        return lax.rem(at + (d % n), n)

    def nb(axis, d):
        i = idx(axis, d)
        return {"z": {"depth": i}, "y": {"col": i}, "x": {"row": 2 * i + c}}[axis]

    partner = {"row": 2 * x + (1 - c)}

    def at(i, size):
        return pl.ds(pl.multiple_of(i * size, size), size)

    def block(full, core, o, part=None):
        rows = at(core, tk) if part is None else pl.ds(pl.multiple_of(core * tk + part * half, half), half)
        return full.at[rows, at(idx("y", o), hb)]

    def wblock(o, core):
        return bw1.at[at(2 * idx("x", o) + core, hr), :]

    def piece(d, o):
        return bw2.at[at(idx("z", d), fz), at(idx("y", o), hb)]

    stores = []

    def store(src, dst):
        copy = pltpu.make_async_copy(src, dst, osem.at[len(stores)])
        stores.append(copy)
        copy.start()

    def mark(key):
        plan.msg(key, ("l", key), 0)
        return key

    loads = {}

    def load(name, src, dst):
        loads[name] = pltpu.make_async_copy(src, dst, lsem.at[len(loads)])
        plan.task(len(loads) / 10, [], [mark(name)], loads[name].wait, COST["mid"])

    load("s", w2_ref.at[at(z, fz), :], vw2)
    load("w", w1_ref.at[:, at(c, fc)], wblock(0, c))
    load("x", x_ref, block(bx, c, 0))
    load("g", g_ref, block(bg, c, 0))
    self_copy = pltpu.make_async_copy(w2_ref.at[at(z, fz), :], piece(0, 0), lsem.at[len(loads)])

    def raw(prio, waits, keys):
        plan.task(prio, waits, keys, lambda: comm.start(*keys), COST["go"], raw=True)

    def passed(prio, wait, keys, key=None):
        plan.task(prio, [wait], [*keys, mark(("in", *wait) if key is None else key)], lambda: comm.start(*keys), COST["go"])

    for o in (1, -1, 2, 0):
        o = o % ny
        to = {"row": 2 * idx("x", o) + c, "col": x}
        comm.msg(("s", o), ("t", 0), lambda: vw2, lambda: piece(0, 0), to, mail=(y, idx("y", o)))
    comm.remote_if[("s", 0)] = x != y
    plan.task(1, ["s"], [("s", o) for o in range(ny)], lambda: comm.start(*[("s", o) for o in range(ny)]), COST["go"])
    whole = {d: [] for d in range(nz)}
    far = nz // 2
    for o in range(ny):
        for w in ways:
            steps = far if (w > 0) == (o % 2 == 0) else far - 1
            for t in range(steps):
                comm.msg(("z", o, w, t), ("z", w), lambda o=o, w=w, t=t: piece(-w * t, o), lambda o=o, w=w, t=t: piece(-w * t, o), nb("z", w))
                nxt = [("z", o, w, t + 1)] if t + 1 < steps else []
                key = ("w2", o, (-w * (t + 1)) % nz)
                passed(4, ("z", o, w, t), nxt, key)
                whole[key[2]].append(key)
        first = [("z", o, w, 0) for w in ways]

        def slice_in(o=o, first=first):
            if o == 0:
                pl.when(x == y)(self_copy.wait)
            comm.start(*first)

        plan.task(3, [("s", o)], [*first, mark(("w2", o, 0))], slice_in, COST["go"])
        whole[0].append(("w2", o, 0))

    comm.msg(("pw",), ("d", 0), lambda: w1_ref.at[:, at(1 - c, fc)], lambda: wblock(0, c), partner)
    raw(1.1, [], [("pw",)])
    w1_in = {0: ["w"], 1: [], -1: [], 2: []}
    for own in (True, False):
        core = c if own else 1 - c
        for w in ways:
            comm.msg(("wa", own, w), ("x", w), lambda core=core: wblock(0, core), lambda core=core: wblock(0, core), nb("x", w))
    raw(1.2, ["w"], [("wa", True, w) for w in ways])
    passed(5, ("pw",), [("wa", False, w) for w in ways])
    w1_in[0].append(("in", "pw"))
    for own, w in ((True, 1), (False, -1)):
        core = c if own else 1 - c
        comm.msg(("wf", w), ("x", w), lambda core=core, w=w: wblock(-w, core), lambda core=core, w=w: wblock(-w, core), nb("x", w))
        passed(6, ("wa", own, w), [("wf", w)])
        passed(6, ("wa", not own, w), [])
        passed(6, ("wf", w), [])
        w1_in[-w] += [("in", "wa", True, w), ("in", "wa", False, w)]
        w1_in[2].append(("in", "wf", w))

    arrived = {}
    for a, (full, name) in enumerate(((bx, "x"), (bg, "g"))):
        arrived[a] = [name]
        for w in ways:
            for p in range(2):
                comm.msg((name, w, p), ("y", w), lambda full=full, p=p: block(full, c, 0, p), lambda full=full, p=p: block(full, c, 0, p), nb("y", w))
            p = 0 if w > 0 else 1
            comm.msg((name, "f", w), ("y", w), lambda full=full, w=w, p=p: block(full, c, -w, p), lambda full=full, w=w, p=p: block(full, c, -w, p), nb("y", w))

        def share(key, o, p, full=full, name=name, a=a):
            comm.msg((name, "d", *key), ("d", 0), lambda: block(full, c, o, p), lambda: block(full, c, o, p), partner)
            passed(20, (name, "d", *key), [])
            arrived[a].append(("in", name, "d", *key))
            return (name, "d", *key)

        plan.task(2 + a, [name], [share((0,), 0, None)], lambda name=name: comm.start((name, "d", 0)), COST["go"])
        for w in ways:
            p = 0 if w > 0 else 1
            for q in range(2):
                keys = [share((-w, q), -w, q)] + ([(name, "f", w)] if q == p else [])
                passed(7, (name, w, q), keys)
                arrived[a].append(("in", name, w, q))
            passed(7, (name, "f", w), [share((2, p), 2, p)])
            arrived[a].append(("in", name, "f", w))
    for n, (name, late) in enumerate(itertools.product("xg", (False, True))):
        raw(1.3 + n / 100, [name], [(name, w, 1 if (w > 0) == late else 0) for w in ways])
    plan.task(9, arrived[0], [mark("X")], lambda: store(bx, xf), COST["go"])
    near = [key for key in arrived[1] if not (key[:3] == ("in", "g", "f") or key[:4] == ("in", "g", "d", 2))]
    plan.task(9, near, [mark("G3")], lambda: None, COST["go"])
    plan.task(9, arrived[1], [mark("G")], lambda: store(bg, gf), COST["go"])

    tile = 256
    order_u = (0, 1, -1, 2)
    for n, o in enumerate(order_u):
        def up(n=n, o=o):
            j = idx("x", o)
            store(bw1.at[at(j, hb), :], w1f.at[at(j, hb), :])

            @pl.loop(0, 2 * fc // tile)
            def _(i):
                rows, cols = at(lax.rem(i, 2), tk), at(lax.div(i, 2), tile)
                v = mm(bx[rows, at(j, hb)], bw1[at(j, hb), cols])
                u[rows, cols] = v if n == 0 else u[rows, cols] + v

        plan.task(30, ["X", *w1_in[o], *([("U", n - 1)] if n else [])], [mark(("U", n))], up, COST["U"])
    for d in sorted(range(nz), key=lambda d: min(d, nz - d)):
        def down(os, d=d):
            cols = at(idx("z", d), fz)

            @pl.loop(0, 2)
            def _(i):
                rows = at(i, tk)
                v = sum(mm_t(bg[rows, at(idx("y", o), hb)], bw2[cols, at(idx("y", o), hb)]) for o in os)
                da[rows, cols] = v if len(os) > 1 else da[rows, cols] + v

        def act(d=d):
            cols = at(idx("z", d), fz)

            @pl.loop(0, 2 * tk // fz)
            def _(i):
                rows = at(i, fz)
                h, vjp = jax.vjp(gelu_fn, u[rows, cols])
                ha[rows, cols] = h.astype(BF16)
                hd[rows, cols] = vjp(da[rows, cols])[0].astype(BF16)

            store(bw2.at[cols, :], w2f.at[cols, :])
            store(ha.at[:, cols], hid.at[:, cols])
            store(hd.at[:, cols], dpre.at[:, cols])

        plan.task(31, ["G3", *whole[d]], [mark(("A3", d))], functools.partial(down, (0, 1, -1)), COST["A3"])
        plan.task(32, ["G", ("A3", d)], [mark(("A", d))], functools.partial(down, (2,)), COST["A"])
        plan.task(33, [("A", d), ("U", len(order_u) - 1)], [], act, COST["act"])

    order = plan.order()
    for copy in loads.values():
        copy.start()
    pl.when(x == y)(self_copy.start)

    barrier = pltpu.get_barrier_semaphore()

    def tell(to):
        pl.semaphore_signal(barrier, inc=1, device_id=to, device_id_type=MESH)

    for to in (*[nb(axis, d) for axis in "zyx" for d in ways], partner):
        tell(to)
    for o in range(1, ny):
        tell({"row": 2 * y + c, "col": idx("y", o)})
    pl.when(x != y)(lambda: tell({"row": 2 * y + c, "col": y}))
    pl.semaphore_wait(barrier, 6 + ny + jnp.where(x != y, 1, 0))
    run_tasks(plan, comm, order)
    for copy in stores:
        copy.wait()


def gather(dims, tok, grad, up, down):
    tk, hb = tok.shape
    fc = down.shape[0]
    nz, ny, nx = dims
    sds, vm = jax.ShapeDtypeStruct, pltpu.VMEM
    tokens, first, second, mid = (2 * tk, ny * hb), (nx * hb, fc), (fc, ny * hb), (2 * tk, fc)
    return pl.pallas_call(
        functools.partial(gather_kernel, dims),
        out_shape=[sds(shape, BF16) for shape in (tokens, tokens, first, second, mid, mid)],
        in_specs=[ANY] * 4,
        out_specs=[ANY] * 6,
        scratch_shapes=[
            *[vm(shape, BF16) for shape in (tokens, tokens, first, second, (fc // nz, hb))],
            vm(mid, F32),
            vm(mid, F32),
            vm(mid, BF16),
            vm(mid, BF16),
            pltpu.SemaphoreType.DMA((80,)),
            pltpu.SemaphoreType.DMA((80,)),
            pltpu.SemaphoreType.DMA((5,)),
            pltpu.SemaphoreType.DMA((30,)),
        ],
        compiler_params=pltpu.CompilerParams(collective_id=0, has_side_effects=True, vmem_limit_bytes=VMEM_LIMIT),
        name="gather",
    )(tok, grad, up, down)


def reduce_kernel(dims, tok, grad, up, down, hid, dpre,
                  y_out, dx_out, g1_out, g2_out, dwp, yp, wx1, wx2, hx, dx, *scratch):
    nz, ny, nx = dims
    z, y, x, c = where_am_i()
    hb = y_out.shape[-1]
    tk = tok.shape[0] // 2
    hr = hb // 2
    fc = hid.shape[1]
    nu = fc // (nz * 8)
    sgn = (1, -1)
    scratch = list(scratch)

    def grab(n):
        return [scratch.pop(0) for _ in range(n)]

    nc = len(CHUNKS)
    xbuf, zbuf, tbuf = grab(nc), grab(nc), grab(nc)
    o1, o2, yr, yo, lhs, par, tmp = grab(7)
    pools = grab(5)
    ssem, rsem, lsem, osem, isem, tsem = grab(6)
    P_X, P_Z, P_Y, P_R, P_W = range(5)

    plan = Plan(RATES, WINDOW)
    comm = Comm(plan, ssem, rsem)

    def idx(axis, d):
        at, n = {"z": (z, nz), "y": (y, ny), "x": (x, nx)}[axis]
        return lax.rem(at + (d % n), n)

    def nb(axis, d):
        i = idx(axis, d)
        return {"z": {"depth": i}, "y": {"col": i}, "x": {"row": 2 * i + c}}[axis]

    partner = {"row": 2 * x + (1 - c)}
    across = {"row": 2 * y + c, "col": x}

    def hcol(j):
        return pl.ds(pl.multiple_of(j * hb, hb), hb)

    staged, stores, place = [], [], {}

    def stage(pool, src, marks=(), n=None):
        staged.append((pool, src, tuple(marks), n))
        return len(staged) - 1

    def slot(k):
        return place[k][0]

    def mark(key):
        plan.msg(key, ("l", key), 0)
        return key

    def chain(key, axis, n, s, buf, src, pool, marks, prio, end, end_sends, units=None):
        far, near = n // 2, n // 2 - 1
        for t in range(far):
            comm.msg((key, "F", t), (axis, s), (lambda: src(far * s)) if t == 0 else (lambda t=t: buf.at[t - 1]), lambda t=t: buf.at[t], nb(axis, s))
        for t in range(near):
            comm.msg((key, "N", t), (axis, -s), (lambda: src(-near * s)) if t == 0 else (lambda t=t: buf.at[far + t - 1]), lambda t=t: buf.at[far + t], nb(axis, -s))

        def own(rel):
            return [] if pool is None else [stage(pool, lambda: src(rel), marks(rel), units)]

        def mid(name, t, at, rel):
            ks = own(rel)

            def run():
                accumulate(buf.at[at], [slot(ks[0]) if ks else src(rel)])
                comm.start((key, name, t + 1))

            plan.task(prio, [(key, name, t), *marks(rel)], [(key, name, t + 1)], run, COST["mid"], stage=ks)

        for t in range(far - 1):
            mid("F", t, t, (far - 1 - t) * s)
        for t in range(near - 1):
            mid("N", t, far + t, -(near - 1 - t) * s)
        ks = own(0)
        last = [buf.at[far - 1], buf.at[far + near - 1]]
        plan.task(prio, [(key, "F", far - 1), (key, "N", near - 1), *marks(0)], end_sends,
                  lambda: end(last, slot(ks[0]) if ks else src(0)), COST["fin"], stage=ks)
        return [(key, "F", 0), (key, "N", 0)]

    def raw(prio, marks, keys):
        plan.task(prio, marks, keys, lambda: comm.start(*keys), COST["go"], raw=True)

    def spread(key, s, region, finish):
        far, near = nz // 2, nz // 2 - 1
        for name, count, d in (("GF", far, s), ("GN", near, -s)):
            for t in range(count):
                def ref(t=t, d=d):
                    return region(idx("z", -t * d))
                comm.msg((key, name, t), ("z", d), ref, ref, nb("z", d))
        for name, count in (("GF", far), ("GN", near)):
            for t in range(count - 1):
                plan.task(4, [(key, name, t)], [(key, name, t + 1)], lambda name=name, t=t: comm.start((key, name, t + 1)), COST["go"])
        plan.task(30, [(key, "GF", far - 1), (key, "GN", near - 1)], [], finish, COST["go"])
        return [(key, "GF", 0), (key, "GN", 0)]

    def store(src, dst):
        copy = pltpu.make_async_copy(src, dst, osem.at[len(stores)])
        stores.append(copy)
        copy.start()

    def none(rel):
        return ()

    for i, (a, first_axis, sigma, u, n, prio) in enumerate(CHUNKS):
        s = sgn[sigma]

        def done(o, a=a, u=u, n=n):
            return [("D", a, o % nx, v) for v in range(u, u + n)]

        if a == 0:
            def region(k, u=u, n=n):
                return o1.at[:, pl.ds(u, n), k]

            go = spread(("g", i), s, region, lambda u=u, n=n: store(o1.at[:, pl.ds(u, n)], g1_out.at[:, pl.ds(u, n)]))
            over = ("sw", i)
            comm.msg(over, ("d", 0), lambda i=i: tbuf[i], lambda u=u, n=n: o1.at[c, pl.ds(u, n), z], partner)

            def end(last, own, i=i, u=u, n=n, over=over):
                mine = pl.ds(pl.multiple_of(c * hr, hr), hr)
                other = pl.ds(pl.multiple_of((1 - c) * hr, hr), hr)
                for m in range(n):
                    tbuf[i][m] = own[m, :, other] + last[0][m, :, other] + last[1][m, :, other]
                comm.start(over)
                for m in range(n):
                    o1[c, u + m, z] = own[m, :, mine] + last[0][m, :, mine] + last[1][m, :, mine]
        else:
            def region(k, u=u, n=n):
                return o2.at[pl.ds(u, n), k]

            go = spread(("g", i), s, region, lambda u=u, n=n: store(o2.at[pl.ds(u, n)], g2_out.at[pl.ds(u, n)]))
            over = ("tr", i)
            comm.msg(over, ("t", 0), lambda i=i: tbuf[i], lambda region=region: region(z), across)
            comm.remote_if[over] = x != y

            def end(last, own, i=i, u=u, n=n, over=over):
                for m in range(n):
                    tbuf[i][m] = own[m] + last[0][m] + last[1][m]
                comm.start(over)

                @pl.when(x == y)
                def _():
                    for m in range(n):
                        o2[u + m, z] = tbuf[i][m]

        plan.task(3, [over], go, lambda go=go: comm.start(*go), COST["go"])
        if first_axis == "x":
            res = xbuf[i].at[nx // 2 - 1]
            raws = chain(("z", i), "z", nz, s, zbuf[i], lambda rel, res=res: res.at[:, idx("z", rel)], None, none, 5, end, [over])

            def x_end(last, own, raws=raws):
                accumulate(last[0], [last[1], own])
                comm.start(*raws)

            raws = chain(("x", i), "x", nx, s, xbuf[i], lambda rel, a=a, u=u, n=n: dwp.at[a, pl.ds(u, n), :, :, hcol(idx("x", rel))],
                         P_X, lambda rel, done=done: done(rel), 10, x_end, raws, n)
            raw(11 + prio / 100, done(2) + done(-s), raws)
        else:
            res = zbuf[i].at[nz // 2 - 1]
            raws = chain(("x", i), "x", nx, s, xbuf[i], lambda rel, res=res: res.at[:, :, hcol(idx("x", rel))], None, none, 8, end, [over])

            def z_end(last, own, raws=raws):
                accumulate(last[0], [last[1], own])
                comm.start(*raws)

            all_done = [m for o in range(nx) for m in done(o)]
            raws = chain(("z", i), "z", nz, s, zbuf[i], lambda rel, a=a, u=u, n=n: dwp.at[a, pl.ds(u, n), idx("z", rel)],
                         P_Z, lambda rel, all_done=all_done: all_done, 9, z_end, raws, n)
            raw(11 + prio / 100, all_done, raws)

    groups = yo.shape[1]
    for a, out in enumerate((y_out, dx_out)):
        for sigma in range(2):
            s = sgn[sigma]
            half = pl.ds(sigma * (groups // 2), groups // 2)

            def y_end(last, own, a=a, half=half, sigma=sigma, out=out):
                def one(ix):
                    yo[(a, sigma * (groups // 2) + ix[0], ix[1])] = (own[ix] + last[0][ix] + last[1][ix]).astype(BF16)

                each(own.shape, one)
                store(yo.at[a, half], out.at[half])

            raws = chain(("y", a, sigma), "y", ny, s, yr.at[a, sigma], lambda rel, a=a, half=half: yp.at[a, half, :, :, hcol(idx("y", rel))],
                         P_Y, lambda rel, a=a: [("Y", a, rel % ny)], 12, y_end, [])
            raw(11, [("Y", a, 2), ("Y", a, -s % ny)], raws)

    tile = 256

    def rows(o):
        return pl.ds(pl.multiple_of(idx("y", o) * hb, hb), hb)

    def arrive(key, prio=6):
        plan.task(prio, [key], [mark(("got", *key))], lambda: None, 0.01)
        return ("got", *key)

    lhs_loads = [pltpu.make_async_copy(src, lhs.at[n], isem.at[n]) for n, src in enumerate((hid, dpre))]
    for n in (0, 1):
        plan.task(0, [], [mark(("T", n))], lhs_loads[n].wait, 0.3)

    others = pl.ds(pl.multiple_of((1 - c) * tk, tk), tk)
    own_rows = pl.ds(pl.multiple_of(c * tk, tk), tk)
    par_loads = []
    for n, (src, box) in enumerate(((hid, hx), (dpre, dx))):
        comm.msg(("hx", n), ("d", 0), lambda src=src: src.at[others], lambda box=box: box, partner)
        raw(1, [], [("hx", n)])
        par_loads.append(pltpu.make_async_copy(box, par.at[n], isem.at[2 + n]))
        plan.task(6, [("hx", n)], [mark(("P", n))], par_loads[n].start, 0.02)
    for a, o in Y_ORDER:
        if a == 0:
            comm.msg(("w", a, o), ("d", 0), lambda o=o: down.at[:, hcol(idx("y", o))], lambda o=o: wx2.at[:, hcol(idx("y", o))], partner)
        else:
            comm.msg(("w", a, o), ("d", 0), lambda o=o: up.at[rows(o)], lambda o=o: wx1.at[rows(o)], partner)
        raw(2, [], [("w", a, o)])

    par_seen = set()
    last_of, b = {}, 1
    for n, job in enumerate(JOBS):
        opens, closes = job[0] == "D" or job[3] == 0, job[0] == "D" or job[3] == 1
        b = 1 - b if opens else b
        keys = [("Y", job[1], job[2])] if job[0] == "Y" else [("D", job[1], job[2] % nx, v) for v in range(job[3], job[3] + job[4])]
        span = pl.ds(0, yo.shape[1] if job[0] == "Y" else job[4])
        waits = [("C", n - 1)] if n else []
        if opens and b in last_of:
            waits.append(("S", last_of[b]))
        if job[0] == "D":
            _, a, o, u, n_u = job
            waits.append(("T", 1 - a))
            ks = [stage(P_R, lambda a=a, o=o: (tok, grad)[a].at[:, hcol(idx("x", o))])]

            def value(cols, a=a, u=u, n_u=n_u, ks=ks):
                return mm_l(lhs[1 - a, :, u * nz * 8:(u + n_u) * nz * 8], slot(ks[0])[:, cols])

            dst = functools.partial(lambda a, o, u, n_u: dwp.at[a, pl.ds(u, n_u), :, :, hcol(idx("x", o))], a, o, u, n_u)
            cost = COST["D"][n_u]
        else:
            _, a, o, h = job
            waits.append(("T", a))
            marks = []
            if h:
                marks = [arrive(("w", a, o))]
                waits += [("P", a), *marks]
            if a == 0:
                ks = [stage(P_R, lambda o=o, w=(down, wx2)[h]: w.at[:, hcol(idx("y", o))], marks)]
            else:
                ks = [stage(P_W, lambda o=o, w=(up, wx1)[h]: w.at[rows(o)], marks)]

            def value(cols, a=a, h=h, ks=ks):
                left = par[a] if h else lhs[a, own_rows, :]
                return mm(left, slot(ks[0])[:, cols]) if a == 0 else mm_t(left, slot(ks[0])[cols, :])

            dst = functools.partial(lambda a, o: yp.at[a, :, :, :, hcol(idx("y", o))], a, o)
            cost = COST["Y"]

        def save(b=b, dst=dst, span=span):
            return pltpu.make_async_copy(tmp.at[b, span], dst(), tsem.at[b])

        def run(b=b, value=value, save=save, job=job, span=span, opens=opens, closes=closes):
            if job[0] == "Y" and job[3] and job[1] not in par_seen:
                par_loads[job[1]].wait()
                par_seen.add(job[1])

            @pl.loop(0, hb // tile)
            def _(t):
                cols = pl.ds(pl.multiple_of(t * tile, tile), tile)
                v = value(cols).reshape((span.size,) + tmp.shape[2:4] + (tile,))
                tmp[b, span, :, :, cols] = v if opens else tmp[b, span, :, :, cols] + v

            if closes:
                save().start()

        sends = [mark(("C", n))]
        if closes:
            plan.msg(("W", n), ("s", n), 0)
            sends.append(("W", n))
            last_of[b] = n
            plan.task(2, [("W", n)], [mark(("S", n)), *[mark(key) for key in keys]], lambda save=save: save().wait(), 0.03)
        plan.task(40, waits, sends, run, cost, stage=ks)

    order = plan.order()

    at = {}
    for n, i in enumerate(order):
        for w in plan.tasks[i][2]:
            at[w] = n
    uses = {p: [] for p in range(len(pools))}
    user = {}
    for n, i in enumerate(order):
        for k in plan.tasks[i][5]:
            uses[staged[k][0]].append(k)
            user[k] = n
    lbase, fill = 0, {}
    for p, ks in uses.items():
        depth = pools[p].shape[0]
        for n, k in enumerate(ks):
            box = pools[p].at[n % depth] if staged[k][3] is None else pools[p].at[n % depth, pl.ds(0, staged[k][3])]
            place[k] = (box, lsem.at[lbase + n % depth])
            when = -1 if n < depth else user[ks[n - depth]]
            for w in staged[k][2]:
                when = max(when, at[w])
            fill.setdefault(when, []).append(k)
        lbase += depth

    def load(k):
        return pltpu.make_async_copy(staged[k][1](), *place[k])

    for n in LHS_ORDER:
        lhs_loads[n].start()
    for k in fill.get(-1, ()):
        load(k).start()

    barrier = pltpu.get_barrier_semaphore()

    def tell(to):
        pl.semaphore_signal(barrier, inc=1, device_id=to, device_id_type=MESH)

    for to in (*[nb(axis, d) for axis in "zyx" for d in (1, -1)], partner):
        tell(to)

    @pl.when(x != y)
    def _():
        tell(across)

    pl.semaphore_wait(barrier, 7 + jnp.where(x != y, 1, 0))

    run_tasks(plan, comm, order, load, fill)
    for copy in stores:
        copy.wait()


def reduce(dims, tok, grad, up, down, hid, dpre):
    nz, ny, nx = dims
    rows2, hh = tok.shape
    fc = hid.shape[1]
    tk, hb = rows2 // 2, hh // ny
    hr = hb // 2
    nu = fc // (nz * SUB)
    g = tk // (SUB * SUB)
    vm = pltpu.VMEM

    def per(shape):
        return [vm(shape(axis, n), F32) for _, axis, _, _, n, _ in CHUNKS]

    def fin(shape):
        return [vm((n, SUB, hr if a == 0 else hb), F32) for a, _, _, _, n, _ in CHUNKS]

    n0 = max(chunk[4] for chunk in CHUNKS)
    scratch = [
        *per(lambda axis, n: (nx - 1, n, nz, SUB, hb) if axis == "x" else (nx - 1, n, SUB, hb)),
        *per(lambda axis, n: (nz - 1, n, SUB, hb) if axis == "x" else (nz - 1, n, SUB, hh)),
        *fin(0),
        vm((2, nu, nz, SUB, hr), F32),
        vm((nu, nz, SUB, hb), F32),
        vm((2, 2, ny - 1, g // 2, SUB, SUB, hb), F32),
        vm((2, g, SUB, SUB, hb), BF16),
        vm((2, rows2, fc), BF16),
        vm((2, tk, fc), BF16),
        vm((2, g, SUB, SUB, hb), F32),
        vm((3, n0, nz, SUB, hb), F32),
        vm((6, n0, SUB, hh), F32),
        vm((2, g // 2, SUB, SUB, hb), F32),
        vm((3, rows2, hb), BF16),
        vm((3, hb, fc), BF16),
        pltpu.SemaphoreType.DMA((340,)),
        pltpu.SemaphoreType.DMA((340,)),
        pltpu.SemaphoreType.DMA((18,)),
        pltpu.SemaphoreType.DMA((24,)),
        pltpu.SemaphoreType.DMA((6,)),
        pltpu.SemaphoreType.DMA((2,)),
    ]
    sds = jax.ShapeDtypeStruct
    outs = pl.pallas_call(
        functools.partial(reduce_kernel, dims),
        out_shape=[
            sds((g, SUB, SUB, hb), BF16),
            sds((g, SUB, SUB, hb), BF16),
            sds((2, nu, nz, SUB, hr), F32),
            sds((nu, nz, SUB, hb), F32),
            sds((2, nu, nz, SUB, hh), F32),
            sds((2, g, SUB, SUB, hh), F32),
            sds(up.shape, BF16),
            sds(down.shape, BF16),
            sds((tk, fc), BF16),
            sds((tk, fc), BF16),
        ],
        in_specs=[ANY] * 6,
        out_specs=[ANY] * 10,
        scratch_shapes=scratch,
        compiler_params=pltpu.CompilerParams(collective_id=1, has_side_effects=True, vmem_limit_bytes=VMEM_LIMIT),
        name="reduce",
    )(tok, grad, up, down, hid, dpre)
    y, dx, g1, g2 = outs[:4]
    return y.reshape(tk, hb), dx.reshape(tk, hb), g1.reshape(2 * fc, hr).T, g2.reshape(fc, hb)


def solution(mesh):
    act_spec = P(("depth", "row"), "col")
    weight_spec = P("row", "col")
    dims = (mesh.shape["depth"], mesh.shape["col"], mesh.shape["row"] // 2)

    def local_block(tok_blk, up_blk, down_blk, grad_blk):
        return reduce(dims, *gather(dims, tok_blk, grad_blk, up_blk, down_blk))

    return jax.shard_map(local_block, mesh=mesh, in_specs=(act_spec, weight_spec, weight_spec, act_spec), out_specs=(act_spec, act_spec, weight_spec, weight_spec), check_vma=False)
```

time: 962 us -> 330 us (0.34)
  waiting for transfers between devices: 851 us -> 0 us
  Pallas kernels: 0 us -> 317 us
  matrix products: 84.4 us -> 0 us
  between operations: 13.9 us -> 0.66 us
    reduce_scatter x4 -> x0, waiting for transfers between devices: 470 us -> none  [the longest x1 153 us: local_block(): lax.psum_scatter(d_hidden_part, 'col', scatter_dimension=1, tiled=True)]
    pallas_call x0 -> x2, Pallas kernels: none -> 317 us  [the longest x1 227 us: reduce(): pl.pallas_call(functools.partial(reduce_kernel, dims), out_shape=[sds((g,...]
    all_gather x4 -> x0, waiting for transfers between devices: 246 us -> none  [the longest x1 72.8 us: local_block(): down_cols = lax.all_gather(down_blk, 'row', axis=0, tiled=True)]
    psum x1 -> x0, waiting for transfers between devices: 133 us -> none  [local_block(): dw_up = lax.psum(dw_up_layer, 'depth')]
    dot_general x6 -> x0, matrix products: 84.4 us -> none  [the longest x1 16.3 us: local_block(): pre_act = jnp.dot(tok_full, up_cols, preferred_element_type=jnp.float32)]
  transfers between devices with their start and end apart: 9 -> 0, of which waited for: 9 -> 0; matrix products, arithmetic and copies ran while one was open for 7% -> 0% of each run, Pallas kernels for 0% -> 0%
where the time goes in v2:
time: 330 us; the launch traced here: 327 us
  Pallas kernels  317 us (96%)
  local copies, waits for them, and re-layouts  9.49 us (3%)
    pallas_call x1, Pallas kernels, reduce(): pl.pallas_call(functools.partial(reduce_kernel, dims), out_shape=[sds((g,...  227 us
    pallas_call x1, Pallas kernels, gather(): pl.pallas_call(functools.partial(gather_kernel, dims), out_shape=[sds(sha...  89.7 us

profile of v2, /device:TPU:32, one launch (start us, length us, event | category | flops | bytes accessed | tf_op | source)
XLA Modules:
  0.0 326.7 jit_solution(2363693656736415468)
XLA Ops:
  0.6 89.7 %gather.1 = (bf16[1024,3072]{1,0:T(8,128)(2,1)}, bf16[1024,3072]{1,0:T(8,128)(2,1)}, bf16[3072,1024]{1,0:T(8,128)(2,1)}, bf16[1024,3072]{1,0:T(8,128)(2,1)}, bf1...) custom-call(bf16[512,768]{1,0:T(8,128)(2,1)} %x_ref.1, bf16[512,768]{1,0:T(8,128)(2,1)} %g_ref.1, ...), custom_call_target="tpu_custom_call" | custom-call | tf_op jit(solution)/shard_map/gather/pallas_call | solution.py:412
  90.4 226.8 %reduce.1 = (bf16[8,8,8,768]{3,2,1,0:T(8,128)(2,1)}, bf16[8,8,8,768]{3,2,1,0:T(8,128)(2,1)}, f32[2,16,8,8,384]{4,3,2,1,0:T(8,128)}, f32[16,8,8,768]{3,2,1,0:T(8,...) custom-call(bf16[1024,3072]{1,0:T(8,128)(2,1)} %get-tuple-element.14, ...), custom_call_target="tpu_custom_call" | custom-call | tf_op jit(solution)/shard_map/reduce/pallas_call | solution.py:805
  317.2 0.0 copy-start
  317.2 3.7 %copy.8 = f32[2048,384]{0,1:T(8,128)} copy(f32[2048,384]{1,0:T(8,128)} %bitcast.6) | data formatting | bytes 6291456 | tf_op jit(solution)/shard_map/reshape | solution.py:826
  320.9 2.1 copy.12
  322.9 2.1 copy.13
  325.0 0.0 copy-done
  325.0 1.7 copy.14
Async XLA Ops:
  317.2 7.8 %copy-start = (f32[16,8,8,768]{3,2,1,0:T(8,128)S(1)}, f32[16,8,8,768]{3,2,1,0:T(8,128)}, u32[]{:S(2)}) copy-start(f32[16,8,8,768]{3,2,1,0:T(8,128)} %get-tuple-element.23) | copy-start | bytes 9437188

commit v3 on v2

--- a/solution.py
+++ b/solution.py
@@ -14,10 +14,14 @@
 SUB = 8
 BF16 = jnp.bfloat16
 
-CHUNKS = [(1, "z", i % 2, 8 + 2 * i, 2, i) for i in range(4)]
-CHUNKS += [(0, "z", i % 2, 12 + 2 * i, 2, 20 + i) for i in range(2)]
-CHUNKS += [(1, "x", i % 2, 2 * i, 2, i) for i in range(4)]
-CHUNKS += [(0, "x", i % 2, 2 * i, 2, 4 + i) for i in range(6)]
+def chunk_list():
+    def run(a, axis, lo, hi, n, rank):
+        return [(a, axis, k % 2, u, n, rank + k) for k, u in enumerate(range(lo, hi, n))]
+
+    return [*run(1, "z", 8, 16, 2, 0), *run(0, "z", 14, 16, 2, 20), *run(1, "x", 0, 8, 2, 0), *run(0, "x", 0, 12, 2, 4), *run(0, "x", 12, 14, 1, 10)]
+
+
+CHUNKS = chunk_list()
 FAR_FIRST = (2, 1, 3, 0)
 Y_ORDER = [(a, o) for a in range(2) for o in FAR_FIRST]
 
@@ -26,10 +30,9 @@
     def block(a, u, n, order=FAR_FIRST):
         return [("D", a, o, u, n) for o in order]
 
-    head = block(1, 8, 4, range(4)) + block(1, 0, 4) + block(1, 12, 4, range(4))
-    rest = block(1, 4, 4) + block(0, 0, 8) + block(0, 8, 4) + block(0, 12, 4, range(4))
-    both = head + rest
-    cut = len(both) // 2
+    near = range(4)
+    both = block(1, 8, 4, near) + block(1, 0, 4) + block(1, 12, 4, near) + block(1, 4, 4) + block(0, 0, 8) + block(0, 8, 6) + block(0, 14, 2, near)
+    cut = len(both) // 3
     jobs = both[:cut]
     out = [[("Y", a, o, 0), ("Y", a, o, 1)] for a, o in Y_ORDER]
     for job, two in itertools.zip_longest(both[cut:], out):
@@ -39,8 +42,9 @@
 
 JOBS = job_list()
 LHS_ORDER = (0, 1)
-COST = {"D": {2: 0.75, 4: 1.15, 8: 1.57}, "Y": 1.15, "mid": 0.05, "fin": 0.1, "go": 0.03, "U": 3.05, "A3": 1.55, "A": 0.6, "act": 0.63}
+COST = {"D": {2: 0.75, 4: 1.15, 6: 1.4, 8: 1.57}, "Y": 1.15, "mid": 0.05, "fin": 0.1, "go": 0.03, "U": 4.0, "A": 0.8, "act": 3.0}
 SLACK = 40.0
+SPREAD, GATED = 11.5, True
 VMEM_LIMIT = 66_500_000
 
 
@@ -96,8 +100,9 @@
         return out
 
 
-RATES = {"x": (42e3, 2.2), "y": (44e3, 2.2), "z": (45e3, 2.2), "d": (300e3, 3.0), "t": (42e3, 5.0), "l": (1e12, 0.0), "s": (1e12, 1.5)}
-WINDOW = 6.0
+RATES = {axis: (45e3, 2.2) for axis in "xyz"}
+RATES.update(d=(450e3, 3.0), t=(45e3, 5.0), l=(1e12, 0.0), s=(1e12, 2.0))
+WINDOW = 10.0
 
 
 class Comm:
@@ -178,12 +183,13 @@
         rest(None)
 
 
+def total(refs, ix):
+    return functools.reduce(lambda a, b: a + b, [ref[ix] for ref in refs])
+
+
 def accumulate(dst, others):
     def one(ix):
-        total = dst[ix]
-        for o in others:
-            total = total + o[ix]
-        dst[ix] = total
+        dst[ix] = total([dst, *others], ix)
 
     each(dst.shape, one)
 
@@ -201,7 +207,7 @@
 
 
 def gather_kernel(dims, x_ref, g_ref, w1_ref, w2_ref, xf, gf, w1f, w2f, hid, dpre,
-                  bx, bg, bw1, bw2, vw2, u, da, ha, hd, ssem, rsem, lsem, osem):
+                  bx, bg, bw1, bw2, vw2, u, da, ha, hd, ssem, rsem, lsem, osem, asem):
     nz, ny, nx = dims
     z, y, x, c = where_am_i()
     tk, hb = x_ref.shape
@@ -333,54 +339,60 @@
                 arrived[a].append(("in", name, w, q))
             passed(7, (name, "f", w), [share((2, p), 2, p)])
             arrived[a].append(("in", name, "f", w))
-    for n, (name, late) in enumerate(itertools.product("xg", (False, True))):
+    for n, (name, late) in enumerate(itertools.product("gx", (False, True))):
         raw(1.3 + n / 100, [name], [(name, w, 1 if (w > 0) == late else 0) for w in ways])
-    plan.task(9, arrived[0], [mark("X")], lambda: store(bx, xf), COST["go"])
-    near = [key for key in arrived[1] if not (key[:3] == ("in", "g", "f") or key[:4] == ("in", "g", "d", 2))]
-    plan.task(9, near, [mark("G3")], lambda: None, COST["go"])
-    plan.task(9, arrived[1], [mark("G")], lambda: store(bg, gf), COST["go"])
+    for name, here, src, dst in (("X", arrived[0], bx, xf), ("G", arrived[1], bg, gf), ("W2", [key for d in whole for key in whole[d]], bw2, w2f),
+                                 ("W1", [key for o in w1_in for key in w1_in[o]], bw1, w1f)):
+        plan.task(9, here, [mark(name)], functools.partial(store, src, dst), COST["go"])
 
     tile = 256
-    order_u = (0, 1, -1, 2)
-    for n, o in enumerate(order_u):
-        def up(n=n, o=o):
-            j = idx("x", o)
-            store(bw1.at[at(j, hb), :], w1f.at[at(j, hb), :])
-
-            @pl.loop(0, 2 * fc // tile)
-            def _(i):
-                rows, cols = at(lax.rem(i, 2), tk), at(lax.div(i, 2), tile)
-                v = mm(bx[rows, at(j, hb)], bw1[at(j, hb), cols])
-                u[rows, cols] = v if n == 0 else u[rows, cols] + v
-
-        plan.task(30, ["X", *w1_in[o], *([("U", n - 1)] if n else [])], [mark(("U", n))], up, COST["U"])
-    for d in sorted(range(nz), key=lambda d: min(d, nz - d)):
-        def down(os, d=d):
-            cols = at(idx("z", d), fz)
-
-            @pl.loop(0, 2)
-            def _(i):
-                rows = at(i, tk)
-                v = sum(mm_t(bg[rows, at(idx("y", o), hb)], bw2[cols, at(idx("y", o), hb)]) for o in os)
-                da[rows, cols] = v if len(os) > 1 else da[rows, cols] + v
-
-        def act(d=d):
-            cols = at(idx("z", d), fz)
-
-            @pl.loop(0, 2 * tk // fz)
-            def _(i):
-                rows = at(i, fz)
-                h, vjp = jax.vjp(gelu_fn, u[rows, cols])
-                ha[rows, cols] = h.astype(BF16)
-                hd[rows, cols] = vjp(da[rows, cols])[0].astype(BF16)
-
-            store(bw2.at[cols, :], w2f.at[cols, :])
-            store(ha.at[:, cols], hid.at[:, cols])
-            store(hd.at[:, cols], dpre.at[:, cols])
-
-        plan.task(31, ["G3", *whole[d]], [mark(("A3", d))], functools.partial(down, (0, 1, -1)), COST["A3"])
-        plan.task(32, ["G", ("A3", d)], [mark(("A", d))], functools.partial(down, (2,)), COST["A"])
-        plan.task(33, [("A", d), ("U", len(order_u) - 1)], [], act, COST["act"])
+
+    e = lax.rem(y - x + ny, ny)
+    early = lax.div(e, 2) * (3 - e), 1 + 2 * lax.div(e, 2)
+    late = 2, 4 - early[0] - early[1]
+
+    def up(ts, first):
+        js = [lax.rem(x + t, nx) for t in ts]
+
+        @pl.loop(0, fc // tile)
+        def _(i):
+            cols = at(i, tile)
+            v = sum(mm(bx[:, at(j, hb)], bw1[at(j, hb), cols]) for j in js)
+            u[:, cols] = v if first else u[:, cols] + v
+
+    near = ["w", *[key for key in w1_in[0] + w1_in[1] + w1_in[-1]], *[key for key in arrived[0] if not (key[:3] == ("in", "x", "f") or key[:4] == ("in", "x", "d", 2))]]
+    plan.task(30, near, [mark(("U", 0))], functools.partial(up, early, True), COST["U"])
+    plan.task(30, [("U", 0), "X", "W1"], [mark(("U", 1))], functools.partial(up, late, False), COST["U"])
+
+    def down(ds):
+        spans = [at(idx("z", d), fz) for d in ds]
+
+        @pl.loop(0, 2)
+        def _(i):
+            rows = at(i, tk)
+            v = mm_t(bg[rows, :], jnp.concatenate([bw2[span, :] for span in spans]))
+            for n, span in enumerate(spans):
+                da[rows, span] = v[:, n * fz:(n + 1) * fz]
+
+    for d in range(far + 1):
+        ds = sorted({d, -d % nz})
+        plan.task(31, ["G", *[key for e in ds for key in whole[e]]], [mark(("A", d))], functools.partial(down, ds), COST["A"] * len(ds) + 1)
+
+    parts = 2 * tk // tile
+    acts = [pltpu.make_async_copy(src, dst, asem.at[n]) for n, (src, dst) in enumerate(((ha, hid), (hd, dpre)))]
+
+    def act():
+        @pl.loop(0, parts * (fc // fz))
+        def _(i):
+            rows, cols = at(lax.rem(i, parts), tile), at(lax.div(i, parts), fz)
+            h, vjp = jax.vjp(gelu_fn, u[rows, cols])
+            ha[rows, cols] = h.astype(BF16)
+            hd[rows, cols] = vjp(da[rows, cols])[0].astype(BF16)
+
+        for copy in acts:
+            copy.start()
+
+    plan.task(32, [("U", 1), *[("A", d) for d in range(far + 1)]], [], act, COST["act"])
 
     order = plan.order()
     for copy in loads.values():
@@ -399,7 +411,7 @@
     pl.when(x != y)(lambda: tell({"row": 2 * y + c, "col": y}))
     pl.semaphore_wait(barrier, 6 + ny + jnp.where(x != y, 1, 0))
     run_tasks(plan, comm, order)
-    for copy in stores:
+    for copy in [*stores, *acts]:
         copy.wait()
 
 
@@ -423,7 +435,8 @@
             pltpu.SemaphoreType.DMA((80,)),
             pltpu.SemaphoreType.DMA((80,)),
             pltpu.SemaphoreType.DMA((5,)),
-            pltpu.SemaphoreType.DMA((30,)),
+            pltpu.SemaphoreType.DMA((9,)),
+            pltpu.SemaphoreType.DMA((2,)),
         ],
         compiler_params=pltpu.CompilerParams(collective_id=0, has_side_effects=True, vmem_limit_bytes=VMEM_LIMIT),
         name="gather",
@@ -523,7 +536,7 @@
                 comm.msg((key, name, t), ("z", d), ref, ref, nb("z", d))
         for name, count in (("GF", far), ("GN", near)):
             for t in range(count - 1):
-                plan.task(4, [(key, name, t)], [(key, name, t + 1)], lambda name=name, t=t: comm.start((key, name, t + 1)), COST["go"])
+                plan.task(SPREAD, [(key, name, t)], [(key, name, t + 1)], lambda name=name, t=t: comm.start((key, name, t + 1)), COST["go"], raw=GATED)
         plan.task(30, [(key, "GF", far - 1), (key, "GN", near - 1)], [], finish, COST["go"])
         return [(key, "GF", 0), (key, "GN", 0)]
 
@@ -553,10 +566,10 @@
                 mine = pl.ds(pl.multiple_of(c * hr, hr), hr)
                 other = pl.ds(pl.multiple_of((1 - c) * hr, hr), hr)
                 for m in range(n):
-                    tbuf[i][m] = own[m, :, other] + last[0][m, :, other] + last[1][m, :, other]
+                    tbuf[i][m] = total([own, *last], (m, slice(None), other))
                 comm.start(over)
                 for m in range(n):
-                    o1[c, u + m, z] = own[m, :, mine] + last[0][m, :, mine] + last[1][m, :, mine]
+                    o1[c, u + m, z] = total([own, *last], (m, slice(None), mine))
         else:
             def region(k, u=u, n=n):
                 return o2.at[pl.ds(u, n), k]
@@ -568,7 +581,7 @@
 
             def end(last, own, i=i, u=u, n=n, over=over):
                 for m in range(n):
-                    tbuf[i][m] = own[m] + last[0][m] + last[1][m]
+                    tbuf[i][m] = total([own, *last], m)
                 comm.start(over)
 
                 @pl.when(x == y)
@@ -576,10 +589,11 @@
                     for m in range(n):
                         o2[u + m, z] = tbuf[i][m]
 
-        plan.task(3, [over], go, lambda go=go: comm.start(*go), COST["go"])
+        plan.task(SPREAD, [over], go, lambda go=go: comm.start(*go), COST["go"], raw=GATED)
         if first_axis == "x":
             res = xbuf[i].at[nx // 2 - 1]
-            raws = chain(("z", i), "z", nz, s, zbuf[i], lambda rel, res=res: res.at[:, idx("z", rel)], None, none, 5, end, [over])
+            pieces = functools.partial(lambda res, rel: res.at[:, idx("z", rel)], res)
+            raws = chain(("z", i), "z", nz, s, zbuf[i], pieces, None, none, 5, end, [over])
 
             def x_end(last, own, raws=raws):
                 accumulate(last[0], [last[1], own])
@@ -609,7 +623,7 @@
 
             def y_end(last, own, a=a, half=half, sigma=sigma, out=out):
                 def one(ix):
-                    yo[(a, sigma * (groups // 2) + ix[0], ix[1])] = (own[ix] + last[0][ix] + last[1][ix]).astype(BF16)
+                    yo[(a, sigma * (groups // 2) + ix[0], ix[1])] = total([own, *last], ix).astype(BF16)
 
                 each(own.shape, one)
                 store(yo.at[a, half], out.at[half])
@@ -624,7 +638,8 @@
         return pl.ds(pl.multiple_of(idx("y", o) * hb, hb), hb)
 
     def arrive(key, prio=6):
-        plan.task(prio, [key], [mark(("got", *key))], lambda: None, 0.01)
+        plan.msg(("got", *key), ("s", key), 0)
+        plan.task(prio, [key], [("got", *key)], lambda: None, COST["go"])
         return ("got", *key)
 
     lhs_loads = [pltpu.make_async_copy(src, lhs.at[n], isem.at[n]) for n, src in enumerate((hid, dpre))]
@@ -747,14 +762,11 @@
     def tell(to):
         pl.semaphore_signal(barrier, inc=1, device_id=to, device_id_type=MESH)
 
-    for to in (*[nb(axis, d) for axis in "zyx" for d in (1, -1)], partner):
+    peers = [*[nb(axis, d) for axis in "zyx" for d in sgn], partner]
+    for to in peers:
         tell(to)
-
-    @pl.when(x != y)
-    def _():
-        tell(across)
-
-    pl.semaphore_wait(barrier, 7 + jnp.where(x != y, 1, 0))
+    pl.when(x != y)(lambda: tell(across))
+    pl.semaphore_wait(barrier, len(peers) + jnp.where(x != y, 1, 0))
 
     run_tasks(plan, comm, order, load, fill)
     for copy in stores:
@@ -772,10 +784,10 @@
     vm = pltpu.VMEM
 
     def per(shape):
-        return [vm(shape(axis, n), F32) for _, axis, _, _, n, _ in CHUNKS]
+        return [vm(shape(axis, n), F32) for _, axis, _, _, n, *_ in CHUNKS]
 
     def fin(shape):
-        return [vm((n, SUB, hr if a == 0 else hb), F32) for a, _, _, _, n, _ in CHUNKS]
+        return [vm((n, SUB, hr if a == 0 else hb), F32) for a, _, _, _, n, *_ in CHUNKS]
 
     n0 = max(chunk[4] for chunk in CHUNKS)
     scratch = [
@@ -823,7 +835,54 @@
         name="reduce",
     )(tok, grad, up, down, hid, dpre)
     y, dx, g1, g2 = outs[:4]
-    return y.reshape(tk, hb), dx.reshape(tk, hb), g1.reshape(2 * fc, hr).T, g2.reshape(fc, hb)
+    return finish(y.reshape(tk, hb), dx.reshape(tk, hb), g1.reshape(2 * fc, hr), g2.reshape(fc, hb))
+
+
+def finish_kernel(*refs):
+    *arrays, turned, isem, osem = refs
+    n, parts = isem.shape
+    ins, outs, boxes = (arrays[k * n:(k + 1) * n] for k in range(3))
+
+    def span(ref, k):
+        size = ref.shape[0] // parts
+        return pl.ds(k * size, size)
+
+    def fetch(i, k):
+        return pltpu.make_async_copy(ins[i].at[span(ins[i], k)], boxes[i].at[span(ins[i], k)], isem.at[i, k])
+
+    def put(i, k):
+        if i == 0:
+            cols = span(ins[i], k)
+            return pltpu.make_async_copy(turned.at[:, cols], outs[i].at[:, cols], osem.at[i, k])
+        return pltpu.make_async_copy(boxes[i].at[span(ins[i], k)], outs[i].at[span(ins[i], k)], osem.at[i, k])
+
+    todo = list(itertools.product(range(n), range(parts)))
+    for i, k in todo:
+        fetch(i, k).start()
+    for i, k in todo:
+        fetch(i, k).wait()
+        if i == 0:
+            rows = span(ins[i], k)
+            turned[:, rows] = boxes[i][rows, :].T
+        put(i, k).start()
+    for i, k in todo:
+        put(i, k).wait()
+
+
+def finish(y, dx, g1, g2):
+    ins = (g1, g2, y, dx)
+    turned = jax.ShapeDtypeStruct(g1.shape[::-1], F32)
+    parts = 4
+    out = pl.pallas_call(
+        finish_kernel,
+        out_shape=[turned, *[jax.ShapeDtypeStruct(v.shape, v.dtype) for v in ins[1:]]],
+        in_specs=[ANY] * len(ins),
+        out_specs=[ANY] * len(ins),
+        scratch_shapes=[*[pltpu.VMEM(v.shape, v.dtype) for v in ins], pltpu.VMEM(turned.shape, F32), *[pltpu.SemaphoreType.DMA((len(ins), parts))] * 2],
+        compiler_params=pltpu.CompilerParams(vmem_limit_bytes=VMEM_LIMIT),
+        name="finish",
+    )(*ins)
+    return out[2], out[3], out[0], out[1]
 
 
 def solution(mesh):

time: 330 us -> 313 us (0.948); the launches traced: 327 us -> 313 us
  local copies, waits for them, and re-layouts: 9.49 us -> 0 us
  Pallas kernels: 317 us -> 312 us
    pallas_call x1, Pallas kernels: 89.7 us -> 82.6 us  [gather(): pl.pallas_call(functools.partial(gather_kernel, dims), out_shape=[sds(sha...]
    pallas_call x0 -> x1, Pallas kernels: none -> 6.39 us  [finish(): pl.pallas_call(finish_kernel, out_shape=[turned, *[jax.ShapeDtypeStruct(v...]
    unnamed x5 -> x0, local copies, waits for them, and re-layouts: 5.79 us -> none
    reshape x1 -> x0, local copies, waits for them, and re-layouts: 3.7 us -> none  [reduce(): g1.reshape(2 * fc, hr)]
    pallas_call x1, Pallas kernels: 227 us -> 223 us  [reduce(): pl.pallas_call(functools.partial(reduce_kernel, dims), out_shape=[sds((g,...]
where the time goes in v3:
time: 313 us
  Pallas kernels  312 us (100%)
    pallas_call x1, Pallas kernels, reduce(): pl.pallas_call(functools.partial(reduce_kernel, dims), out_shape=[sds((g,...  223 us
    pallas_call x1, Pallas kernels, gather(): pl.pallas_call(functools.partial(gather_kernel, dims), out_shape=[sds(sha...  82.6 us
    pallas_call x1, Pallas kernels, finish(): pl.pallas_call(finish_kernel, out_shape=[turned, *[jax.ShapeDtypeStruct(v...  6.39 us

profile of v3, /device:TPU:32, one launch (start us, length us, event | category | flops | bytes accessed | tf_op | source)
XLA Modules:
  0.0 313.0 jit_solution(8043870975538770974)
XLA Ops:
  0.6 82.6 %gather.1 = (bf16[1024,3072]{1,0:T(8,128)(2,1)}, bf16[1024,3072]{1,0:T(8,128)(2,1)}, bf16[3072,1024]{1,0:T(8,128)(2,1)}, bf16[1024,3072]{1,0:T(8,128)(2,1)}, bf1...) custom-call(bf16[512,768]{1,0:T(8,128)(2,1)} %x_ref.1, bf16[512,768]{1,0:T(8,128)(2,1)} %g_ref.1, ...), custom_call_target="tpu_custom_call" | custom-call | tf_op jit(solution)/shard_map/gather/pallas_call | solution.py:424
  83.3 223.1 %reduce.1 = (bf16[8,8,8,768]{3,2,1,0:T(8,128)(2,1)}, bf16[8,8,8,768]{3,2,1,0:T(8,128)(2,1)}, f32[2,16,8,8,384]{4,3,2,1,0:T(8,128)}, f32[16,8,8,768]{3,2,1,0:T(8,...) custom-call(bf16[1024,3072]{1,0:T(8,128)(2,1)} %get-tuple-element.18, ...), custom_call_target="tpu_custom_call" | custom-call | tf_op jit(solution)/shard_map/reduce/pallas_call | solution.py:817
  306.4 6.4 %finish.1 = (f32[384,2048]{1,0:T(8,128)}, f32[1024,768]{1,0:T(8,128)}, bf16[512,768]{1,0:T(8,128)(2,1)}, bf16[512,768]{1,0:T(8,128)(2,1)}) custom-call(f32[2048,384]{1,0:T(8,128)} %bitcast.4, f32[1024,768]{1,0:T(8,128)} %bitcast.5, bf16[512,768]{1,0:T(8,128)(2,1)} %bitcast.6, bf16[512,768]{1,0:T(8,128)(2,1)} %bitcast.7), custom_call_target="tpu_custom_call" | custom-call | tf_op jit(solution)/shard_map/finish/pallas_call | solution.py:876

commit v4 on v3

--- a/solution.py
+++ b/solution.py
@@ -14,11 +14,16 @@
 SUB = 8
 BF16 = jnp.bfloat16
 
+TOP = (12, 10)
+UNITS = 16
+
+
 def chunk_list():
-    def run(a, axis, lo, hi, n, rank):
-        return [(a, axis, k % 2, u, n, rank + k) for k, u in enumerate(range(lo, hi, n))]
-
-    return [*run(1, "z", 8, 16, 2, 0), *run(0, "z", 14, 16, 2, 20), *run(1, "x", 0, 8, 2, 0), *run(0, "x", 0, 12, 2, 4), *run(0, "x", 12, 14, 1, 10)]
+    def run(a, axis, lo, hi, rank):
+        return [(a, axis, k % 2, u, min(2, hi - u), rank + k) for k, u in enumerate(range(lo, hi, 2))]
+
+    first, last = TOP
+    return [*run(1, "z", last, UNITS, 0), *run(0, "z", first, UNITS, 20), *run(0, "x", 0, first, 0), *run(1, "x", 0, last - 1, 6), (1, "x", 1, last - 1, 1, 11)]
 
 
 CHUNKS = chunk_list()
@@ -27,24 +32,26 @@
 
 
 def job_list():
-    def block(a, u, n, order=FAR_FIRST):
-        return [("D", a, o, u, n) for o in order]
-
-    near = range(4)
-    both = block(1, 8, 4, near) + block(1, 0, 4) + block(1, 12, 4, near) + block(1, 4, 4) + block(0, 0, 8) + block(0, 8, 6) + block(0, 14, 2, near)
-    cut = len(both) // 3
-    jobs = both[:cut]
+    def block(a, lo, hi):
+        return [("D", a, o, u, min(4, hi - u)) for u in range(lo, hi, 4) for o in FAR_FIRST]
+
+    z_first = block(1, TOP[1], UNITS)
+    rest = block(0, 0, TOP[0]) + block(1, 0, TOP[1])
+    both = rest[:3] + z_first[:4] + rest[3:4] + z_first[4:] + rest[4:]
+    half = len(both) // 2
+    both[half:half] = block(0, TOP[0], UNITS)
+    cut = int(0.7 * len(both))
+    jobs, both = both[:cut], both[cut:]
     out = [[("Y", a, o, 0), ("Y", a, o, 1)] for a, o in Y_ORDER]
-    for job, two in itertools.zip_longest(both[cut:], out):
-        jobs += ([job] if job else []) + (two or [])
+    while both or out:
+        jobs, both = jobs + both[:3], both[3:]
+        jobs += out.pop(0) if out else []
     return jobs
 
 
 JOBS = job_list()
-LHS_ORDER = (0, 1)
-COST = {"D": {2: 0.75, 4: 1.15, 6: 1.4, 8: 1.57}, "Y": 1.15, "mid": 0.05, "fin": 0.1, "go": 0.03, "U": 4.0, "A": 0.8, "act": 3.0}
-SLACK = 40.0
-SPREAD, GATED = 11.5, True
+COST = {"D": (0.5, 0.15), "Y": 1.2, "fin": 0.1, "go": 0.03, "U": 4.0, "A": 0.8, "act": 3.0}
+SLACK = 20.0
 VMEM_LIMIT = 66_500_000
 
 
@@ -87,11 +94,12 @@
             for s in self.tasks[i][2]:
                 rate, lat = self.rates[self.link[s][0]]
                 took = self.size[s] / rate
-                if self.link[s][0] == "t":
+                if self.link[s][0] in "to":
+                    share = 0.5 if self.link[s][0] == "t" else 1.5
                     ways = [(axis, d) for axis in "xy" for d in (1, -1)]
                     done = max(now, *[free.get(way, 0.0) for way in ways]) + took
                     for way in ways:
-                        free[way] = max(now, free.get(way, 0.0)) + took / 2
+                        free[way] = max(now, free.get(way, 0.0)) + took * share
                 else:
                     done = max(now, free.get(self.link[s], 0.0)) + took
                     free[self.link[s]] = done
@@ -101,23 +109,27 @@
 
 
 RATES = {axis: (45e3, 2.2) for axis in "xyz"}
-RATES.update(d=(450e3, 3.0), t=(45e3, 5.0), l=(1e12, 0.0), s=(1e12, 2.0))
-WINDOW = 10.0
+RATES.update(d=(450e3, 3.0), t=(45e3, 5.0), o=(45e3, 7.0), l=(1e12, 0.0), s=(1e12, 2.0))
+WINDOW = 8.0
 
 
 class Comm:
     def __init__(self, plan, ssem, rsem):
         self.plan, self.ssem, self.rsem = plan, ssem, rsem
-        self.make, self.meet, self.slot, self.remote_if, self.flying = {}, {}, {}, {}, []
-
-    def msg(self, key, link, src, dst, to, mail=None):
+        self.make, self.meet, self.slot, self.remote_if, self.groups, self.grouped, self.flying = {}, {}, {}, {}, {}, set(), []
+
+    def msg(self, key, link, src, dst, to, mail=None, group=None):
         i = len(self.slot)
         self.slot[key] = i
         there, here = mail or (i, i)
+        name, ref = group or (key, None)
+        g, _, _ = self.groups.setdefault(name, (len(self.groups), ref, to))
+        if group:
+            self.grouped.add(key)
 
         def make(r):
             return pltpu.make_async_remote_copy(
-                src_ref=src(), dst_ref=dst(), send_sem=self.ssem.at[i], recv_sem=self.rsem.at[r], device_id=to, device_id_type=MESH)
+                src_ref=src(), dst_ref=dst(), send_sem=self.ssem.at[g], recv_sem=self.rsem.at[r], device_id=to, device_id_type=MESH)
 
         self.make[key] = lambda: make(there)
         self.meet[key] = lambda: make(here)
@@ -133,8 +145,14 @@
                 act(make[key]())
 
     def start(self, *keys):
-        self.flying.extend(keys)
+        self.flying.extend(key for key in keys if key not in self.grouped)
         self.each(keys, self.make, lambda copy: copy.start())
+
+    def finish(self):
+        self.sent(float("inf"))
+        for g, ref, to in self.groups.values():
+            if ref is not None:
+                pltpu.make_async_remote_copy(src_ref=ref, dst_ref=ref, send_sem=self.ssem.at[g], recv_sem=self.rsem.at[g], device_id=to, device_id_type=MESH).wait_send()
 
     def wait(self, *keys):
         self.each(keys, self.meet, lambda copy: copy.wait_recv())
@@ -145,10 +163,13 @@
         self.each(keys, self.make, lambda copy: copy.wait_send())
 
 
-def run_tasks(plan, comm, order, load=None, fill={}):
+def run_tasks(plan, comm, order, ready, load=None, fill={}):
     heard = set()
     for n, i in enumerate(order):
-        _, waits, _, run, _, ks, _ = plan.tasks[i]
+        _, waits, sends, run, _, ks, _ = plan.tasks[i]
+        if ready and any(key in comm.make for key in sends):
+            ready()
+            ready = None
         with jax.named_scope(f"w{n}"):
             comm.wait(*[w for w in waits if w not in heard])
             heard.update(waits)
@@ -160,7 +181,7 @@
         for k in fill.get(n, ()):
             load(k).start()
         comm.sent(plan.when[n] - SLACK)
-    comm.sent(float("inf"))
+    comm.finish()
 
 
 def where_am_i():
@@ -255,7 +276,7 @@
 
     def load(name, src, dst):
         loads[name] = pltpu.make_async_copy(src, dst, lsem.at[len(loads)])
-        plan.task(len(loads) / 10, [], [mark(name)], loads[name].wait, COST["mid"])
+        plan.task(len(loads) / 10, [], [mark(name)], loads[name].wait, COST["go"])
 
     load("s", w2_ref.at[at(z, fz), :], vw2)
     load("w", w1_ref.at[:, at(c, fc)], wblock(0, c))
@@ -409,8 +430,7 @@
     for o in range(1, ny):
         tell({"row": 2 * y + c, "col": idx("y", o)})
     pl.when(x != y)(lambda: tell({"row": 2 * y + c, "col": y}))
-    pl.semaphore_wait(barrier, 6 + ny + jnp.where(x != y, 1, 0))
-    run_tasks(plan, comm, order)
+    run_tasks(plan, comm, order, lambda: pl.semaphore_wait(barrier, 6 + ny + jnp.where(x != y, 1, 0)))
     for copy in [*stores, *acts]:
         copy.wait()
 
@@ -498,9 +518,9 @@
     def chain(key, axis, n, s, buf, src, pool, marks, prio, end, end_sends, units=None):
         far, near = n // 2, n // 2 - 1
         for t in range(far):
-            comm.msg((key, "F", t), (axis, s), (lambda: src(far * s)) if t == 0 else (lambda t=t: buf.at[t - 1]), lambda t=t: buf.at[t], nb(axis, s))
+            comm.msg((key, "F", t), (axis, s), (lambda: src(far * s)) if t == 0 else (lambda t=t: buf.at[t - 1]), lambda t=t: buf.at[t], nb(axis, s), group=(key, buf))
         for t in range(near):
-            comm.msg((key, "N", t), (axis, -s), (lambda: src(-near * s)) if t == 0 else (lambda t=t: buf.at[far + t - 1]), lambda t=t: buf.at[far + t], nb(axis, -s))
+            comm.msg((key, "N", t), (axis, -s), (lambda: src(-near * s)) if t == 0 else (lambda t=t: buf.at[far + t - 1]), lambda t=t: buf.at[far + t], nb(axis, -s), group=(key, buf))
 
         def own(rel):
             return [] if pool is None else [stage(pool, lambda: src(rel), marks(rel), units)]
@@ -512,7 +532,7 @@
                 accumulate(buf.at[at], [slot(ks[0]) if ks else src(rel)])
                 comm.start((key, name, t + 1))
 
-            plan.task(prio, [(key, name, t), *marks(rel)], [(key, name, t + 1)], run, COST["mid"], stage=ks)
+            plan.task(prio, [(key, name, t), *marks(rel)], [(key, name, t + 1)], run, COST["go"], stage=ks)
 
         for t in range(far - 1):
             mid("F", t, t, (far - 1 - t) * s)
@@ -527,16 +547,16 @@
     def raw(prio, marks, keys):
         plan.task(prio, marks, keys, lambda: comm.start(*keys), COST["go"], raw=True)
 
-    def spread(key, s, region, finish):
+    def spread(key, s, region, finish, some):
         far, near = nz // 2, nz // 2 - 1
         for name, count, d in (("GF", far, s), ("GN", near, -s)):
             for t in range(count):
                 def ref(t=t, d=d):
                     return region(idx("z", -t * d))
-                comm.msg((key, name, t), ("z", d), ref, ref, nb("z", d))
+                comm.msg((key, name, t), ("z", d), ref, ref, nb("z", d), group=(key, some))
         for name, count in (("GF", far), ("GN", near)):
             for t in range(count - 1):
-                plan.task(SPREAD, [(key, name, t)], [(key, name, t + 1)], lambda name=name, t=t: comm.start((key, name, t + 1)), COST["go"], raw=GATED)
+                plan.task(4, [(key, name, t)], [(key, name, t + 1)], lambda name=name, t=t: comm.start((key, name, t + 1)), COST["go"])
         plan.task(30, [(key, "GF", far - 1), (key, "GN", near - 1)], [], finish, COST["go"])
         return [(key, "GF", 0), (key, "GN", 0)]
 
@@ -558,7 +578,7 @@
             def region(k, u=u, n=n):
                 return o1.at[:, pl.ds(u, n), k]
 
-            go = spread(("g", i), s, region, lambda u=u, n=n: store(o1.at[:, pl.ds(u, n)], g1_out.at[:, pl.ds(u, n)]))
+            go = spread(("g", i), s, region, lambda u=u, n=n: store(o1.at[:, pl.ds(u, n)], g1_out.at[:, pl.ds(u, n)]), o1.at[:, pl.ds(0, n), pl.ds(0, nz - 1)])
             over = ("sw", i)
             comm.msg(over, ("d", 0), lambda i=i: tbuf[i], lambda u=u, n=n: o1.at[c, pl.ds(u, n), z], partner)
 
@@ -574,9 +594,9 @@
             def region(k, u=u, n=n):
                 return o2.at[pl.ds(u, n), k]
 
-            go = spread(("g", i), s, region, lambda u=u, n=n: store(o2.at[pl.ds(u, n)], g2_out.at[pl.ds(u, n)]))
+            go = spread(("g", i), s, region, lambda u=u, n=n: store(o2.at[pl.ds(u, n)], g2_out.at[pl.ds(u, n)]), o2.at[pl.ds(0, n), pl.ds(0, nz - 1)])
             over = ("tr", i)
-            comm.msg(over, ("t", 0), lambda i=i: tbuf[i], lambda region=region: region(z), across)
+            comm.msg(over, ("o", 0), lambda i=i: tbuf[i], lambda region=region: region(z), across)
             comm.remote_if[over] = x != y
 
             def end(last, own, i=i, u=u, n=n, over=over):
@@ -589,7 +609,7 @@
                     for m in range(n):
                         o2[u + m, z] = tbuf[i][m]
 
-        plan.task(SPREAD, [over], go, lambda go=go: comm.start(*go), COST["go"], raw=GATED)
+        plan.task(3, [over], go, lambda go=go: comm.start(*go), COST["go"])
         if first_axis == "x":
             res = xbuf[i].at[nx // 2 - 1]
             pieces = functools.partial(lambda res, rel: res.at[:, idx("z", rel)], res)
@@ -643,23 +663,23 @@
         return ("got", *key)
 
     lhs_loads = [pltpu.make_async_copy(src, lhs.at[n], isem.at[n]) for n, src in enumerate((hid, dpre))]
-    for n in (0, 1):
-        plan.task(0, [], [mark(("T", n))], lhs_loads[n].wait, 0.3)
+    for n in (1, 0):
+        plan.task(0, [], [mark(("T", n))], lhs_loads[n].wait, COST["fin"])
 
     others = pl.ds(pl.multiple_of((1 - c) * tk, tk), tk)
     own_rows = pl.ds(pl.multiple_of(c * tk, tk), tk)
     par_loads = []
     for n, (src, box) in enumerate(((hid, hx), (dpre, dx))):
         comm.msg(("hx", n), ("d", 0), lambda src=src: src.at[others], lambda box=box: box, partner)
-        raw(1, [], [("hx", n)])
+        raw(1, [("C", 3)], [("hx", n)])
         par_loads.append(pltpu.make_async_copy(box, par.at[n], isem.at[2 + n]))
-        plan.task(6, [("hx", n)], [mark(("P", n))], par_loads[n].start, 0.02)
+        plan.task(6, [("hx", n)], [mark(("P", n))], par_loads[n].start, COST["go"])
     for a, o in Y_ORDER:
         if a == 0:
-            comm.msg(("w", a, o), ("d", 0), lambda o=o: down.at[:, hcol(idx("y", o))], lambda o=o: wx2.at[:, hcol(idx("y", o))], partner)
+            comm.msg(("w", a, o), ("d", 0), lambda o=o: down.at[:, hcol(idx("y", o))], lambda o=o: wx2.at[:, hcol(idx("y", o))], partner, group=("w2", wx2))
         else:
-            comm.msg(("w", a, o), ("d", 0), lambda o=o: up.at[rows(o)], lambda o=o: wx1.at[rows(o)], partner)
-        raw(2, [], [("w", a, o)])
+            comm.msg(("w", a, o), ("d", 0), lambda o=o: up.at[rows(o)], lambda o=o: wx1.at[rows(o)], partner, group=("w1", wx1))
+        raw(2, [("C", 3)], [("w", a, o)])
 
     par_seen = set()
     last_of, b = {}, 1
@@ -680,7 +700,7 @@
                 return mm_l(lhs[1 - a, :, u * nz * 8:(u + n_u) * nz * 8], slot(ks[0])[:, cols])
 
             dst = functools.partial(lambda a, o, u, n_u: dwp.at[a, pl.ds(u, n_u), :, :, hcol(idx("x", o))], a, o, u, n_u)
-            cost = COST["D"][n_u]
+            cost = COST["D"][0] + COST["D"][1] * n_u
         else:
             _, a, o, h = job
             waits.append(("T", a))
@@ -722,7 +742,7 @@
             plan.msg(("W", n), ("s", n), 0)
             sends.append(("W", n))
             last_of[b] = n
-            plan.task(2, [("W", n)], [mark(("S", n)), *[mark(key) for key in keys]], lambda save=save: save().wait(), 0.03)
+            plan.task(2, [("W", n)], [mark(("S", n)), *[mark(key) for key in keys]], lambda save=save: save().wait(), COST["go"])
         plan.task(40, waits, sends, run, cost, stage=ks)
 
     order = plan.order()
@@ -752,8 +772,8 @@
     def load(k):
         return pltpu.make_async_copy(staged[k][1](), *place[k])
 
-    for n in LHS_ORDER:
-        lhs_loads[n].start()
+    for copy in lhs_loads[::-1]:
+        copy.start()
     for k in fill.get(-1, ()):
         load(k).start()
 
@@ -766,9 +786,7 @@
     for to in peers:
         tell(to)
     pl.when(x != y)(lambda: tell(across))
-    pl.semaphore_wait(barrier, len(peers) + jnp.where(x != y, 1, 0))
-
-    run_tasks(plan, comm, order, load, fill)
+    run_tasks(plan, comm, order, lambda: pl.semaphore_wait(barrier, len(peers) + jnp.where(x != y, 1, 0)), load, fill)
     for copy in stores:
         copy.wait()
 
@@ -806,8 +824,8 @@
         vm((2, g // 2, SUB, SUB, hb), F32),
         vm((3, rows2, hb), BF16),
         vm((3, hb, fc), BF16),
-        pltpu.SemaphoreType.DMA((340,)),
-        pltpu.SemaphoreType.DMA((340,)),
+        pltpu.SemaphoreType.DMA((80,)),
+        pltpu.SemaphoreType.DMA((330,)),
         pltpu.SemaphoreType.DMA((18,)),
         pltpu.SemaphoreType.DMA((24,)),
         pltpu.SemaphoreType.DMA((6,)),

time: 313 us -> 305 us (0.974)
  Pallas kernels: 312 us -> 301 us
    pallas_call x1, Pallas kernels: 223 us -> 212 us  [reduce(): pl.pallas_call(functools.partial(reduce_kernel, dims), out_shape=[sds((g,...]
where the time goes in v4:
time: 305 us; the launch traced here: 302 us
  Pallas kernels  301 us (99%)
    pallas_call x1, Pallas kernels, reduce(): pl.pallas_call(functools.partial(reduce_kernel, dims), out_shape=[sds((g,...  212 us
    pallas_call x1, Pallas kernels, gather(): pl.pallas_call(functools.partial(gather_kernel, dims), out_shape=[sds(sha...  82.6 us
    pallas_call x1, Pallas kernels, finish(): pl.pallas_call(finish_kernel, out_shape=[turned, *[jax.ShapeDtypeStruct(v...  6.39 us

profile of v4, /device:TPU:32, one launch (start us, length us, event | category | flops | bytes accessed | tf_op | source)
XLA Modules:
  0.0 302.1 jit_solution(3616312235733702209)
XLA Ops:
  0.6 82.6 %gather.1 = (bf16[1024,3072]{1,0:T(8,128)(2,1)}, bf16[1024,3072]{1,0:T(8,128)(2,1)}, bf16[3072,1024]{1,0:T(8,128)(2,1)}, bf16[1024,3072]{1,0:T(8,128)(2,1)}, bf1...) custom-call(bf16[512,768]{1,0:T(8,128)(2,1)} %x_ref.1, bf16[512,768]{1,0:T(8,128)(2,1)} %g_ref.1, ...), custom_call_target="tpu_custom_call" | custom-call | tf_op jit(solution)/shard_map/gather/pallas_call | solution.py:444
  83.2 212.3 %reduce.1 = (bf16[8,8,8,768]{3,2,1,0:T(8,128)(2,1)}, bf16[8,8,8,768]{3,2,1,0:T(8,128)(2,1)}, f32[2,16,8,8,384]{4,3,2,1,0:T(8,128)}, f32[16,8,8,768]{3,2,1,0:T(8,...) custom-call(bf16[1024,3072]{1,0:T(8,128)(2,1)} %get-tuple-element.18, ...), custom_call_target="tpu_custom_call" | custom-call | tf_op jit(solution)/shard_map/reduce/pallas_call | solution.py:835
  295.6 6.4 %finish.1 = (f32[384,2048]{1,0:T(8,128)}, f32[1024,768]{1,0:T(8,128)}, bf16[512,768]{1,0:T(8,128)(2,1)}, bf16[512,768]{1,0:T(8,128)(2,1)}) custom-call(f32[2048,384]{1,0:T(8,128)} %bitcast.4, f32[1024,768]{1,0:T(8,128)} %bitcast.5, bf16[512,768]{1,0:T(8,128)(2,1)} %bitcast.6, bf16[512,768]{1,0:T(8,128)(2,1)} %bitcast.7), custom_call_target="tpu_custom_call" | custom-call | tf_op jit(solution)/shard_map/finish/pallas_call | solution.py:894

commit v5 on v4

--- a/solution.py
+++ b/solution.py
@@ -1,5 +1,6 @@
 import functools
 import itertools
+import string
 
 import jax
 import jax.numpy as jnp
@@ -16,37 +17,33 @@
 
 TOP = (12, 10)
 UNITS = 16
-
-
-def chunk_list():
-    def run(a, axis, lo, hi, rank):
-        return [(a, axis, k % 2, u, min(2, hi - u), rank + k) for k, u in enumerate(range(lo, hi, 2))]
-
-    first, last = TOP
-    return [*run(1, "z", last, UNITS, 0), *run(0, "z", first, UNITS, 20), *run(0, "x", 0, first, 0), *run(1, "x", 0, last - 1, 6), (1, "x", 1, last - 1, 1, 11)]
-
-
-CHUNKS = chunk_list()
 FAR_FIRST = (2, 1, 3, 0)
 Y_ORDER = [(a, o) for a in range(2) for o in FAR_FIRST]
+DIGITS = string.digits + string.ascii_letters
+JOB_ORDER = "10svut2y64z3w5x8rdho9b7AqcfamCBpilgFEnGejkDH"
+RANKS = "107kl30b24216589a"
+SIDES = "01010010101011001"
+
+
+def chunk_list():
+    def run(a, axis, lo, hi, n=2):
+        return [(a, axis, u, min(n, hi - u)) for u in range(lo, hi, n)]
+
+    first, last = TOP
+    parts = run(1, "z", last, UNITS) + run(0, "z", first, UNITS) + run(0, "x", 0, first) + run(1, "x", 0, last - 2) + run(1, "x", last - 2, last, 1)
+    return [(a, axis, int(side), u, n, DIGITS.index(rank)) for (a, axis, u, n), side, rank in zip(parts, SIDES, RANKS)]
+
+
+CHUNKS = chunk_list()
 
 
 def job_list():
     def block(a, lo, hi):
-        return [("D", a, o, u, min(4, hi - u)) for u in range(lo, hi, 4) for o in FAR_FIRST]
-
-    z_first = block(1, TOP[1], UNITS)
-    rest = block(0, 0, TOP[0]) + block(1, 0, TOP[1])
-    both = rest[:3] + z_first[:4] + rest[3:4] + z_first[4:] + rest[4:]
-    half = len(both) // 2
-    both[half:half] = block(0, TOP[0], UNITS)
-    cut = int(0.7 * len(both))
-    jobs, both = both[:cut], both[cut:]
-    out = [[("Y", a, o, 0), ("Y", a, o, 1)] for a, o in Y_ORDER]
-    while both or out:
-        jobs, both = jobs + both[:3], both[3:]
-        jobs += out.pop(0) if out else []
-    return jobs
+        return [[("D", a, o, u, min(4, hi - u))] for u in range(lo, hi, 4) for o in FAR_FIRST]
+
+    first, last = TOP
+    jobs = block(0, 0, first) + block(1, 0, last) + block(0, first, UNITS) + block(1, last, UNITS) + [[("Y", a, o, h) for h in range(2)] for a, o in Y_ORDER]
+    return [job for c in JOB_ORDER for job in jobs[DIGITS.index(c)]]
 
 
 JOBS = job_list()
@@ -110,7 +107,7 @@
 
 RATES = {axis: (45e3, 2.2) for axis in "xyz"}
 RATES.update(d=(450e3, 3.0), t=(45e3, 5.0), o=(45e3, 7.0), l=(1e12, 0.0), s=(1e12, 2.0))
-WINDOW = 8.0
+WINDOW = 10.0
 
 
 class Comm:
@@ -399,19 +396,20 @@
         ds = sorted({d, -d % nz})
         plan.task(31, ["G", *[key for e in ds for key in whole[e]]], [mark(("A", d))], functools.partial(down, ds), COST["A"] * len(ds) + 1)
 
-    parts = 2 * tk // tile
-    acts = [pltpu.make_async_copy(src, dst, asem.at[n]) for n, (src, dst) in enumerate(((ha, hid), (hd, dpre)))]
+    parts = tk // tile
+    acts = [[pltpu.make_async_copy(src.at[at(h, tk), :], dst.at[at(h, tk), :], asem.at[h, n]) for n, (src, dst) in enumerate(((ha, hid), (hd, dpre)))] for h in range(2)]
 
     def act():
-        @pl.loop(0, parts * (fc // fz))
-        def _(i):
-            rows, cols = at(lax.rem(i, parts), tile), at(lax.div(i, parts), fz)
-            h, vjp = jax.vjp(gelu_fn, u[rows, cols])
-            ha[rows, cols] = h.astype(BF16)
-            hd[rows, cols] = vjp(da[rows, cols])[0].astype(BF16)
-
-        for copy in acts:
-            copy.start()
+        for half, copies in enumerate(acts):
+            @pl.loop(0, parts * (fc // fz))
+            def _(i):
+                rows, cols = at(half * parts + lax.rem(i, parts), tile), at(lax.div(i, parts), fz)
+                h, vjp = jax.vjp(gelu_fn, u[rows, cols])
+                ha[rows, cols] = h.astype(BF16)
+                hd[rows, cols] = vjp(da[rows, cols])[0].astype(BF16)
+
+            for copy in copies:
+                copy.start()
 
     plan.task(32, [("U", 1), *[("A", d) for d in range(far + 1)]], [], act, COST["act"])
 
@@ -431,7 +429,7 @@
         tell({"row": 2 * y + c, "col": idx("y", o)})
     pl.when(x != y)(lambda: tell({"row": 2 * y + c, "col": y}))
     run_tasks(plan, comm, order, lambda: pl.semaphore_wait(barrier, 6 + ny + jnp.where(x != y, 1, 0)))
-    for copy in [*stores, *acts]:
+    for copy in [*stores, *sum(acts, [])]:
         copy.wait()
 
 
@@ -456,7 +454,7 @@
             pltpu.SemaphoreType.DMA((80,)),
             pltpu.SemaphoreType.DMA((5,)),
             pltpu.SemaphoreType.DMA((9,)),
-            pltpu.SemaphoreType.DMA((2,)),
+            pltpu.SemaphoreType.DMA((2, 2)),
         ],
         compiler_params=pltpu.CompilerParams(collective_id=0, has_side_effects=True, vmem_limit_bytes=VMEM_LIMIT),
         name="gather",

time: 305 us -> 301 us (0.987)
  no operation moved by 1% of the time
where the time goes in v5:
time: 301 us
  Pallas kernels  300 us (100%)
    pallas_call x1, Pallas kernels, reduce(): pl.pallas_call(functools.partial(reduce_kernel, dims), out_shape=[sds((g,...  212 us
    pallas_call x1, Pallas kernels, gather(): pl.pallas_call(functools.partial(gather_kernel, dims), out_shape=[sds(sha...  82 us
    pallas_call x1, Pallas kernels, finish(): pl.pallas_call(finish_kernel, out_shape=[turned, *[jax.ShapeDtypeStruct(v...  6.39 us

profile of v5, /device:TPU:32, one launch (start us, length us, event | category | flops | bytes accessed | tf_op | source)
XLA Modules:
  0.0 300.8 jit_solution(117130660619861878)
XLA Ops:
  0.6 82.0 %gather.1 = (bf16[1024,3072]{1,0:T(8,128)(2,1)}, bf16[1024,3072]{1,0:T(8,128)(2,1)}, bf16[3072,1024]{1,0:T(8,128)(2,1)}, bf16[1024,3072]{1,0:T(8,128)(2,1)}, bf1...) custom-call(bf16[512,768]{1,0:T(8,128)(2,1)} %x_ref.1, bf16[512,768]{1,0:T(8,128)(2,1)} %g_ref.1, ...), custom_call_target="tpu_custom_call" | custom-call | tf_op jit(solution)/shard_map/gather/pallas_call | solution.py:442
  82.7 211.6 %reduce.1 = (bf16[8,8,8,768]{3,2,1,0:T(8,128)(2,1)}, bf16[8,8,8,768]{3,2,1,0:T(8,128)(2,1)}, f32[2,16,8,8,384]{4,3,2,1,0:T(8,128)}, f32[16,8,8,768]{3,2,1,0:T(8,...) custom-call(bf16[1024,3072]{1,0:T(8,128)(2,1)} %get-tuple-element.18, ...), custom_call_target="tpu_custom_call" | custom-call | tf_op jit(solution)/shard_map/reduce/pallas_call | solution.py:833
  294.3 6.4 %finish.1 = (f32[384,2048]{1,0:T(8,128)}, f32[1024,768]{1,0:T(8,128)}, bf16[512,768]{1,0:T(8,128)(2,1)}, bf16[512,768]{1,0:T(8,128)(2,1)}) custom-call(f32[2048,384]{1,0:T(8,128)} %bitcast.4, f32[1024,768]{1,0:T(8,128)} %bitcast.5, bf16[512,768]{1,0:T(8,128)(2,1)} %bitcast.6, bf16[512,768]{1,0:T(8,128)(2,1)} %bitcast.7), custom_call_target="tpu_custom_call" | custom-call | tf_op jit(solution)/shard_map/finish/pallas_call | solution.py:892

commit v6 on v5

--- a/solution.py
+++ b/solution.py
@@ -450,8 +450,8 @@
             vm(mid, F32),
             vm(mid, BF16),
             vm(mid, BF16),
-            pltpu.SemaphoreType.DMA((80,)),
-            pltpu.SemaphoreType.DMA((80,)),
+            pltpu.SemaphoreType.DMA((65,)),
+            pltpu.SemaphoreType.DMA((65,)),
             pltpu.SemaphoreType.DMA((5,)),
             pltpu.SemaphoreType.DMA((9,)),
             pltpu.SemaphoreType.DMA((2, 2)),
@@ -888,7 +888,7 @@
 def finish(y, dx, g1, g2):
     ins = (g1, g2, y, dx)
     turned = jax.ShapeDtypeStruct(g1.shape[::-1], F32)
-    parts = 4
+    parts = 2
     out = pl.pallas_call(
         finish_kernel,
         out_shape=[turned, *[jax.ShapeDtypeStruct(v.shape, v.dtype) for v in ins[1:]]],

time: 301 us -> 300 us (level)
  no operation moved by 1% of the time
where the time goes in v6:
time: 300 us; the launch traced here: 299 us
  Pallas kernels  299 us (100%)
    pallas_call x1, Pallas kernels, reduce(): pl.pallas_call(functools.partial(reduce_kernel, dims), out_shape=[sds((g,...  212 us
    pallas_call x1, Pallas kernels, gather(): pl.pallas_call(functools.partial(gather_kernel, dims), out_shape=[sds(sha...  81.8 us

profile of v6, /device:TPU:32, one launch (start us, length us, event | category | flops | bytes accessed | tf_op | source)
XLA Modules:
  0.0 299.4 jit_solution(17310909553148388496)
XLA Ops:
  0.6 81.8 %gather.1 = (bf16[1024,3072]{1,0:T(8,128)(2,1)}, bf16[1024,3072]{1,0:T(8,128)(2,1)}, bf16[3072,1024]{1,0:T(8,128)(2,1)}, bf16[1024,3072]{1,0:T(8,128)(2,1)}, bf1...) custom-call(bf16[512,768]{1,0:T(8,128)(2,1)} %x_ref.1, bf16[512,768]{1,0:T(8,128)(2,1)} %g_ref.1, ...), custom_call_target="tpu_custom_call" | custom-call | tf_op jit(solution)/shard_map/gather/pallas_call | solution.py:442
  82.4 211.7 %reduce.1 = (bf16[8,8,8,768]{3,2,1,0:T(8,128)(2,1)}, bf16[8,8,8,768]{3,2,1,0:T(8,128)(2,1)}, f32[2,16,8,8,384]{4,3,2,1,0:T(8,128)}, f32[16,8,8,768]{3,2,1,0:T(8,...) custom-call(bf16[1024,3072]{1,0:T(8,128)(2,1)} %get-tuple-element.18, ...), custom_call_target="tpu_custom_call" | custom-call | tf_op jit(solution)/shard_map/reduce/pallas_call | solution.py:833
  294.1 5.2 %finish.1 = (f32[384,2048]{1,0:T(8,128)}, f32[1024,768]{1,0:T(8,128)}, bf16[512,768]{1,0:T(8,128)(2,1)}, bf16[512,768]{1,0:T(8,128)(2,1)}) custom-call(f32[2048,384]{1,0:T(8,128)} %bitcast.4, f32[1024,768]{1,0:T(8,128)} %bitcast.5, bf16[512,768]{1,0:T(8,128)(2,1)} %bitcast.6, bf16[512,768]{1,0:T(8,128)(2,1)} %bitcast.7), custom_call_target="tpu_custom_call" | custom-call | tf_op jit(solution)/shard_map/finish/pallas_call | solution.py:892

commit v7 on v6

--- a/solution.py
+++ b/solution.py
@@ -20,9 +20,9 @@
 FAR_FIRST = (2, 1, 3, 0)
 Y_ORDER = [(a, o) for a in range(2) for o in FAR_FIRST]
 DIGITS = string.digits + string.ascii_letters
-JOB_ORDER = "10svut2y64z3w5x8rdho9b7AqcfamCBpilgFEnGejkDH"
-RANKS = "107kl30b24216589a"
-SIDES = "01010010101011001"
+JOB_ORDER = "01tvus25ywo84xcz7r9dhA6e3qpajbkfBiElCFGDgmHn"
+RANKS = "73l204k52619810ab"
+SIDES = "10010100110010101"
 
 
 def chunk_list():
@@ -107,7 +107,7 @@
 
 RATES = {axis: (45e3, 2.2) for axis in "xyz"}
 RATES.update(d=(450e3, 3.0), t=(45e3, 5.0), o=(45e3, 7.0), l=(1e12, 0.0), s=(1e12, 2.0))
-WINDOW = 10.0
+WINDOW = 9.0
 
 
 class Comm:

time: 300 us -> 301 us (level)
  no operation moved by 1% of the time
where the time goes in v7:
time: 301 us
  Pallas kernels  300 us (100%)
    pallas_call x1, Pallas kernels, reduce(): pl.pallas_call(functools.partial(reduce_kernel, dims), out_shape=[sds((g,...  213 us
    pallas_call x1, Pallas kernels, gather(): pl.pallas_call(functools.partial(gather_kernel, dims), out_shape=[sds(sha...  81.8 us

profile of v7, /device:TPU:32, one launch (start us, length us, event | category | flops | bytes accessed | tf_op | source)
XLA Modules:
  0.0 300.8 jit_solution(7769371119788033273)
XLA Ops:
  0.6 81.8 %gather.1 = (bf16[1024,3072]{1,0:T(8,128)(2,1)}, bf16[1024,3072]{1,0:T(8,128)(2,1)}, bf16[3072,1024]{1,0:T(8,128)(2,1)}, bf16[1024,3072]{1,0:T(8,128)(2,1)}, bf1...) custom-call(bf16[512,768]{1,0:T(8,128)(2,1)} %x_ref.1, bf16[512,768]{1,0:T(8,128)(2,1)} %g_ref.1, ...), custom_call_target="tpu_custom_call" | custom-call | tf_op jit(solution)/shard_map/gather/pallas_call | solution.py:442
  82.4 213.0 %reduce.1 = (bf16[8,8,8,768]{3,2,1,0:T(8,128)(2,1)}, bf16[8,8,8,768]{3,2,1,0:T(8,128)(2,1)}, f32[2,16,8,8,384]{4,3,2,1,0:T(8,128)}, f32[16,8,8,768]{3,2,1,0:T(8,...) custom-call(bf16[1024,3072]{1,0:T(8,128)(2,1)} %get-tuple-element.18, ...), custom_call_target="tpu_custom_call" | custom-call | tf_op jit(solution)/shard_map/reduce/pallas_call | solution.py:833
  295.4 5.2 %finish.1 = (f32[384,2048]{1,0:T(8,128)}, f32[1024,768]{1,0:T(8,128)}, bf16[512,768]{1,0:T(8,128)(2,1)}, bf16[512,768]{1,0:T(8,128)(2,1)}) custom-call(f32[2048,384]{1,0:T(8,128)} %bitcast.4, f32[1024,768]{1,0:T(8,128)} %bitcast.5, bf16[512,768]{1,0:T(8,128)(2,1)} %bitcast.6, bf16[512,768]{1,0:T(8,128)(2,1)} %bitcast.7), custom_call_target="tpu_custom_call" | custom-call | tf_op jit(solution)/shard_map/finish/pallas_call | solution.py:892
